TPU v7x, 16 devices: a 4x2x1 block of a 4x4x8 slice. The times are simulated.
16 devices in a mesh: data: 2 (over y, z), tensor: 8 (over x, core).
Axes of the slice: x: 4, y: 2, z: 1, core: 2. Of those that a mesh axis runs over, the one named last changes fastest.
The devices are a block of a 4x4x8 slice.
Arguments:
- token_ids: int32 [65536], P(('data', 'tensor')), parts along dimension 0
- emb_table: bfloat16 [50304, 512], P('tensor')
- norm_gain: bfloat16 [512], replicated
- w_up: bfloat16 [512, 2048], P(None, 'tensor')
- w_down: bfloat16 [2048, 512], P('tensor')
- grad_out: bfloat16 [65536, 512], P(('data', 'tensor')), parts along dimension 0
Outputs:
- output 1: bfloat16 [65536, 512], P(('data', 'tensor')), parts along dimension 0
- output 2: float32 [100608, 512], P(('data', 'tensor')), parts along dimension 0
- output 3: float32 [1024, 2048], P('data', 'tensor'), parts along dimension 0
- output 4: float32 [4096, 512], P(('data', 'tensor')), parts along dimension 0
There are 2 independent parts. A program takes and returns all parts, laid end to end along the dimension named above; an argument that names none is the same for every part.
All inputs are finite; a program needn't handle non-finite values.
Results may differ from a plain program's by a relative error of at most 0.00554922.
Values are sent between devices in bfloat16 or wider.
A program may use at most 768 MiB of HBM per device.

v0:
```python
import jax
import jax.numpy as jnp
from jax import lax
from jax.sharding import PartitionSpec as P

EPS = 1e-6


def rms_norm(x_rows, gain_f):
    inv_rms = lax.rsqrt(jnp.mean(x_rows * x_rows, axis=-1, keepdims=True) + EPS)
    return x_rows * inv_rms * gain_f


def gelu_tanh(values):
    return jax.nn.gelu(values, approximate=True)


def contract_last(left_op, right_op):
    return lax.dot_general(left_op, right_op, (((1,), (1,)), ((), ())), preferred_element_type=jnp.float32)


def contract_first(left_op, right_op):
    return lax.dot_general(left_op, right_op, (((0,), (0,)), ((), ())), preferred_element_type=jnp.float32)


def solution(mesh):
    tok_spec = P(('data', 'tensor'))
    row_spec = P(('data', 'tensor'), None)

    def local_step(token_ids, emb_shard, norm_gain, w_up, w_down, grad_out):
        vocab_local = emb_shard.shape[0]
        offset = lax.axis_index('tensor') * vocab_local
        ids_all = lax.all_gather(token_ids, 'tensor', tiled=True)
        rel_ids = ids_all - offset
        is_owned = (rel_ids >= 0) & (rel_ids < vocab_local)
        looked_up = jnp.take(emb_shard, jnp.clip(rel_ids, 0, vocab_local - 1), axis=0)
        emb_part = jnp.where(is_owned[:, None], looked_up, jnp.zeros((), looked_up.dtype))
        x_local = lax.psum_scatter(emb_part, 'tensor', scatter_dimension=0, tiled=True)
        x_f = x_local.astype(jnp.float32)
        gain_f = norm_gain.astype(jnp.float32)
        normed_f, norm_back = jax.vjp(lambda x_in: rms_norm(x_in, gain_f), x_f)
        normed = normed_f.astype(jnp.bfloat16)
        normed_all = lax.all_gather(normed, 'tensor', tiled=True)
        pre_act = jnp.dot(normed_all, w_up, preferred_element_type=jnp.float32).astype(jnp.bfloat16)
        act_f, gelu_back = jax.vjp(gelu_tanh, pre_act.astype(jnp.float32))
        hidden = act_f.astype(jnp.bfloat16)
        y_part = jnp.dot(hidden, w_down, preferred_element_type=jnp.float32)
        y_local = lax.psum_scatter(y_part, 'tensor', scatter_dimension=0, tiled=True)
        out_local = (x_f + y_local).astype(jnp.bfloat16)
        grad_all = lax.all_gather(grad_out, 'tensor', tiled=True)
        d_hidden = contract_last(grad_all, w_down)
        d_pre = gelu_back(d_hidden)[0].astype(jnp.bfloat16)
        d_w_down = contract_first(hidden, grad_all)
        d_w_up = contract_first(normed_all, d_pre)
        d_norm_part = contract_last(d_pre, w_up)
        d_norm = lax.psum_scatter(d_norm_part, 'tensor', scatter_dimension=0, tiled=True)
        dx_local = (grad_out.astype(jnp.float32) + norm_back(d_norm)[0]).astype(jnp.bfloat16)
        dx_all = lax.all_gather(dx_local, 'tensor', tiled=True)
        seg_ids = jnp.where(is_owned, rel_ids, vocab_local)
        d_emb = jax.ops.segment_sum(dx_all.astype(jnp.float32), seg_ids, num_segments=vocab_local + 1)[:vocab_local]
        return out_local, d_emb, d_w_up, d_w_down

    return jax.shard_map(
        local_step,
        mesh=mesh,
        in_specs=(tok_spec, P('tensor', None), P(None), P(None, 'tensor'), P('tensor', None), row_spec),
        out_specs=(row_spec, row_spec, P('data', 'tensor'), row_spec),
        check_vma=False,
    )
```

profile of v0, /device:TPU:113, one launch (start us, length us, event | category | flops | bytes accessed | tf_op | source)
XLA Modules:
  0.0 1783.4 jit_solution(5854817317725974574)
XLA Ops:
  7.2 0.0 copy-start
  7.2 0.1 reduce-scatter.4.cloned.1.call-start
  7.3 19.0 %all_gather.12 = s32[32768]{0:T(1024)S(1)} all-gather(s32[4096]{0:T(1024)} %param.6), channel_id=1, replica_groups=mesh['data'=2,'tensor'=8] {'tensor'}, dimensions={0}, use_global_device_ids=true | all-gather | bytes 147456 | tf_op jit(solution)/shard_map/all_gather | solution.py:33
  26.3 0.1 compare_and_fusion.1
  26.4 0.7 subtract_select_fusion
  27.1 136.4 %gather_fusion = bf16[32768,512]{1,0:T(8,128)(2,1)} fusion(bf16[6288,512]{1,0:T(8,128)(2,1)} %param.7, s32[32768]{0:T(1024)S(1)} %get-tuple-element.7), kind=kCustom, calls=%fused_computation | custom fusion | bytes 67239936 | tf_op jit(solution)/shard_map/jit(_take)/gather | solution.py:36
  163.5 23.3 %select_select_fusion = bf16[32768,512]{1,0:T(8,128)(2,1)} fusion(bf16[32768,512]{1,0:T(8,128)(2,1)} %gather_fusion, pred[32768]{0:T(1024)(128)(4,1)S(1)} %get-tuple-element.9, pred[32768]{0:T(1024)(128)(4,1)S(1)} %get-tuple-element.8), kind=kLoop, calls=%fused_computation.20 | loop fusion | flops 33554432 | bytes 67174400 | tf_op jit(solution)/shard_map/jit(_where)/select_n | solution.py:37
  186.8 0.1 reduce-scatter.4.cloned.1.call-update
  186.8 0.1 all-gather.6.cloned.1.call-start
  186.9 0.7 all-gather.6.cloned.1.call-update
  187.6 0.1 all-gather.4.cloned.1.call-start
  187.7 0.0 copy-done.9
  187.7 0.0 copy-start.7
  187.7 171.0 %reduce-scatter.4.cloned.1.call-done = bf16[4096,512]{1,0:T(8,128)(2,1)} async-done(((bf16[32768,512]{1,0:T(8,128)(2,1)}), bf16[4096,512]{1,0:T(8,128)(2,1)}) %reduce-scatter.4.cloned.1.call-update) | async-done | bytes 4194320 | tf_op jit(solution)/shard_map/reduce_scatter | solution.py:38
  358.7 3.1 fusion.14
  361.8 0.0 copy-start.5
  361.8 0.6 copy-done.5
  362.4 0.0 copy-start.3
  362.4 0.6 copy-done.3
  363.0 4.1 fusion.16
  367.2 0.1 all-gather.4.cloned.1.call-update
  367.2 0.4 reduce-scatter.8.cloned.1.call-start
  367.6 145.9 %all-gather.6.cloned.1.call-done = bf16[32768,512]{1,0:T(8,128)(2,1)} async-done(((bf16[4096,512]{1,0:T(8,128)(2,1)}), bf16[32768,512]{1,0:T(8,128)(2,1)}) %all-gather.6.cloned.1.call-update) | async-done | bytes 33554448 | tf_op jit(solution)/shard_map/all_gather | solution.py:50
  513.5 0.0 copy-done.2
  513.5 26.3 %fusion.26 = f32[32768,256]{1,0:T(8,128)} fusion(bf16[32768,512]{1,0:T(8,128)(2,1)} %all-gather.6.cloned.1.call-done, bf16[256,512]{1,0:T(8,128)(2,1)S(1)} %copy-done.2), kind=kOutput, calls=%fused_computation.45 | convolution fusion | flops 8589934592 | bytes 67371008 | tf_op jit(solution)/shard_map/dot_general | solution.py:19
  539.8 0.0 copy-done.7
  539.8 129.5 %all-gather.4.cloned.1.call-done = bf16[32768,512]{1,0:T(8,128)(2,1)} async-done(((bf16[4096,512]{1,0:T(8,128)(2,1)}), bf16[32768,512]{1,0:T(8,128)(2,1)}) %all-gather.4.cloned.1.call-update) | async-done | bytes 33554448 | tf_op jit(solution)/shard_map/all_gather | solution.py:43
  669.3 0.0 copy-done
  669.3 39.3 %fusion.5 = (bf16[32768,256]{1,0:T(8,128)(2,1)}, bf16[32768,256]{1,0:T(8,128)(2,1)}) fusion(f32[32768,256]{1,0:T(8,128)} %fusion.26, bf16[32768,512]{1,0:T(8,128)(2,1)} %all-gather.4.cloned.1.call-done, bf16[512,256]{1,0:T(8,128)(2,1)S(1)} %copy-done), kind=kOutput, calls=%fused_computation.13 | convolution fusion | flops 8774483968 | bytes 100925440 | tf_op jit(solution)/shard_map/dot_general | solution.py:44
  708.6 29.0 %fusion.27 = f32[32768,512]{1,0:T(8,128)} fusion(bf16[32768,256]{1,0:T(8,128)(2,1)} %get-tuple-element.10, bf16[512,256]{1,0:T(8,128)(2,1)S(1)} %copy-done), kind=kOutput, calls=%fused_computation.46 | convolution fusion | flops 8589934592 | bytes 84148224 | tf_op jit(solution)/shard_map/dot_general | solution.py:19
  737.7 0.1 reduce-scatter.8.cloned.1.call-update
  737.7 0.1 reduce-scatter.6.cloned.1.call-start
  737.8 29.5 %fusion.24 = f32[32768,512]{1,0:T(8,128)} fusion(bf16[256,512]{1,0:T(8,128)(2,1)S(1)} %copy-done.2, bf16[32768,256]{1,0:T(8,128)(2,1)} %get-tuple-element.11), kind=kOutput, calls=%fused_computation.44 | convolution fusion | flops 8673820672 | bytes 84148224 | tf_op jit(solution)/shard_map/dot_general | solution.py:47
  767.3 0.1 reduce-scatter.6.cloned.1.call-update
  767.3 0.1 all-gather.8.cloned.1.call-start
  767.4 294.3 %reduce-scatter.8.cloned.1.call-done = f32[4096,512]{1,0:T(8,128)} async-done(((f32[32768,512]{1,0:T(8,128)}), f32[4096,512]{1,0:T(8,128)}) %reduce-scatter.8.cloned.1.call-update) | async-done | bytes 8388624 | tf_op jit(solution)/shard_map/reduce_scatter | solution.py:56
  1061.7 0.0 copy-done.8
  1061.7 5.8 fusion.18
  1067.5 0.0 copy-done.6
  1067.6 319.8 %reduce-scatter.6.cloned.1.call-done = f32[4096,512]{1,0:T(8,128)} async-done(((f32[32768,512]{1,0:T(8,128)}), f32[4096,512]{1,0:T(8,128)}) %reduce-scatter.6.cloned.1.call-update) | async-done | bytes 8388624 | tf_op jit(solution)/shard_map/reduce_scatter | solution.py:48
  1387.3 0.0 copy-done.4
  1387.3 13.1 fusion.13
  1400.5 0.1 all-gather.8.cloned.1.call-update
  1400.5 20.6 %fusion.28 = f32[512,256]{1,0:T(8,128)} fusion(bf16[32768,512]{1,0:T(8,128)(2,1)} %all-gather.4.cloned.1.call-done, bf16[32768,256]{1,0:T(8,128)(2,1)} %get-tuple-element.10), kind=kOutput, calls=%fused_computation.47 | convolution fusion | flops 8589934592 | bytes 50855936 | tf_op jit(solution)/shard_map/dot_general | solution.py:23
  1421.2 21.9 %fusion.22 = f32[256,512]{1,0:T(8,128)} fusion(bf16[32768,512]{1,0:T(8,128)(2,1)} %all-gather.6.cloned.1.call-done, bf16[32768,256]{1,0:T(8,128)(2,1)} %get-tuple-element.11), kind=kOutput, calls=%fused_computation.43 | convolution fusion | flops 8673820672 | bytes 50855936 | tf_op jit(solution)/shard_map/dot_general | solution.py:23
  1443.1 110.8 %all-gather.8.cloned.1.call-done = bf16[32768,512]{1,0:T(8,128)(2,1)} async-done(((bf16[4096,512]{1,0:T(8,128)(2,1)}), bf16[32768,512]{1,0:T(8,128)(2,1)}) %all-gather.8.cloned.1.call-update) | async-done | bytes 33554448 | tf_op jit(solution)/shard_map/all_gather | solution.py:58
  1553.9 211.4 %scatter_custom_fusion = f32[6289,512]{1,0:T(8,128)} fusion(s32[32768]{0:T(1024)} %get-tuple-element.6, bf16[32768,512]{1,0:T(8,128)(2,1)} %all-gather.8.cloned.1.call-done, f32[]{:T(128)} %constant.22.clone.1), kind=kCustom, calls=%fused_computation.2 | custom fusion | flops 33554432 | bytes 46434816 | tf_op jit(solution)/shard_map/scatter-add | solution.py:60
  1765.2 11.1 slice.6
  (10 shorter events, 0.0 us)
Async XLA Ops:
  7.2 662.1 %copy-start = (bf16[512,256]{1,0:T(8,128)(2,1)S(1)}, bf16[512,256]{1,0:T(8,128)(2,1)}, u32[]{:S(2)}) copy-start(bf16[512,256]{1,0:T(8,128)(2,1)} %param.9) | copy-start | bytes 786436
  7.2 351.5 %reduce-scatter.4.cloned.1.call-start = ((), (), s32[]{:S(2)}) async-start(), calls=%async_computation.3 | async-start | bytes 37748736 | tf_op jit(solution)/shard_map/reduce_scatter | solution.py:38
  186.7 1.0 copy-start.9
  186.7 326.8 %copy-start.2 = (bf16[256,512]{1,0:T(8,128)(2,1)S(1)}, bf16[256,512]{1,0:T(8,128)(2,1)}, u32[]{:S(2)}) copy-start(bf16[256,512]{1,0:T(8,128)(2,1)} %param.10) | copy-start | bytes 786436
  186.8 326.7 %all-gather.6.cloned.1.call-start = ((), (), s32[]{:S(2)}) async-start(), calls=%async_computation.6 | async-start | bytes 37748736 | tf_op jit(solution)/shard_map/all_gather | solution.py:50
  187.6 481.7 %all-gather.4.cloned.1.call-start = ((), (), s32[]{:S(2)}) async-start(), calls=%async_computation.4 | async-start | bytes 37748736 | tf_op jit(solution)/shard_map/all_gather | solution.py:43
  187.7 352.1 %copy-start.7 = (f32[512]{0:T(512)}, f32[512]{0:T(512)S(1)}, u32[]{:S(2)}) copy-start(f32[512]{0:T(512)S(1)} %convert_element_type.34) | copy-start | bytes 6148
  361.8 0.6 copy-start.5
  362.4 0.6 copy-start.3
  367.2 694.5 %reduce-scatter.8.cloned.1.call-start = ((), (), s32[]{:S(2)}) async-start(), calls=%async_computation.7 | async-start | bytes 75497472 | tf_op jit(solution)/shard_map/reduce_scatter | solution.py:56
  737.7 649.6 %reduce-scatter.6.cloned.1.call-start = ((), (), s32[]{:S(2)}) async-start(), calls=%async_computation.5 | async-start | bytes 75497472 | tf_op jit(solution)/shard_map/reduce_scatter | solution.py:48
  767.3 294.4 %copy-start.8 = (f32[512]{0:T(512)S(1)}, f32[512]{0:T(512)}, u32[]{:S(2)}) copy-start(f32[512]{0:T(512)} %copy-done.7) | copy-start | bytes 6148
  767.3 300.3 %copy-start.6 = (f32[4096]{0:T(1024)S(1)}, f32[4096]{0:T(1024)}, u32[]{:S(2)}) copy-start(f32[4096]{0:T(1024)} %copy-done.5) | copy-start | bytes 49156
  767.3 620.1 %copy-start.4 = (f32[4096]{0:T(1024)S(1)}, f32[4096]{0:T(1024)}, u32[]{:S(2)}) copy-start(f32[4096]{0:T(1024)} %copy-done.3) | copy-start | bytes 49156
  767.3 786.5 %all-gather.8.cloned.1.call-start = ((), (), s32[]{:S(2)}) async-start(), calls=%async_computation.8 | async-start | bytes 37748736 | tf_op jit(solution)/shard_map/all_gather | solution.py:58
  1553.9 222.5 %copy-start.1 = (bf16[512,256]{1,0:T(8,128)(2,1)S(1)}, bf16[512,256]{1,0:T(8,128)(2,1)}, u32[]{:S(2)}) copy-start(bf16[512,256]{1,0:T(8,128)(2,1)} %param.9) | copy-start | bytes 786436
Sparse Core Ops, SparseCore 0:
  186.9 171.7 reduce-scatter.3
  360.3 153.1 all-gather.5
  515.7 153.5 all-gather.3
  737.8 323.8 reduce-scatter.7
  1063.9 323.3 reduce-scatter.5
  1400.6 153.1 all-gather.7
where the time goes:
time: 1790 us; the launch traced here: 1780 us
  waiting for transfers between devices  1170 us (65%)
  other arithmetic  262 us (15%)
  matrix products  167 us (9%)
  local copies, waits for them, and re-layouts  149 us (8%)
  blocking collectives  19 us (1%)
    reduce_scatter x1, waiting for transfers between devices, local_step(): lax.psum_scatter(y_part, 'tensor', scatter_dimension=0, tiled=True)  320 us
    reduce_scatter x1, waiting for transfers between devices, local_step(): lax.psum_scatter(d_norm_part, 'tensor', scatter_dimension=0, tiled=True)  294 us
    scatter-add x1, other arithmetic, local_step(): jax.ops.segment_sum(dx_all.astype(jnp.float32), seg_ids, num_segments=voc...  211 us
    reduce_scatter x1, waiting for transfers between devices, local_step(): lax.psum_scatter(emb_part, 'tensor', scatter_dimension=0, tiled=True)  171 us
    all_gather x1, waiting for transfers between devices, local_step(): grad_all = lax.all_gather(grad_out, 'tensor', tiled=True)  146 us
    gather x1, local copies, waits for them, and re-layouts, local_step(): jnp.take(emb_shard, jnp.clip(rel_ids, 0, vocab_local - 1), axis=0)  136 us
    all_gather x1, waiting for transfers between devices, local_step(): normed_all = lax.all_gather(normed, 'tensor', tiled=True)  129 us
    all_gather x1, waiting for transfers between devices, local_step(): dx_all = lax.all_gather(dx_local, 'tensor', tiled=True)  111 us
  transfers between devices with their start and end apart: 6, of which 6 were waited for; matrix products, arithmetic and copies ran while one was open for 6% of the time, Pallas kernels for 0%

commit v1 on v0

v1 whole, which is shorter than its diff:
```python
import functools

import jax
import jax.numpy as jnp
from jax import lax
from jax.experimental import pallas as pl
from jax.experimental.pallas import tpu as pltpu
from jax.sharding import PartitionSpec as P

EPS = 1e-6
F32 = jnp.float32
BF16 = jnp.bfloat16
I32 = jnp.int32
MESH = pl.DeviceIdType.MESH
LANES = 128
UNROLL = 16
PAGE = 1024
AXIS = 'tensor'


def group_barrier(n, me):
    sem = pltpu.get_barrier_semaphore()
    for k in range(1, n):
        pl.semaphore_signal(sem, inc=1, device_id={AXIS: lax.rem(me + k, n)}, device_id_type=MESH)
    pl.semaphore_wait(sem, n - 1)


def far_first(n):
    return sorted(range(1, n), key=lambda k: -min(k // 2, (n - k) // 2))


def blocks(count, size, many, one):
    total = count // size

    def body(b, carry):
        for u in range(many):
            one(pl.multiple_of((b * many + u) * size, size))
        return carry

    lax.fori_loop(0, total // many, body, 0)
    for b in range(total // many * many, total):
        one(b * size)


def split_rows(src, dst, dst_row, count):
    w = src.shape[-1] // LANES

    def one(r0):
        tile = src[pl.ds(r0, 16), :].astype(F32)
        for c in range(w):
            dst[pl.ds((dst_row + r0) * w + c, 16, stride=w), :] = tile[:, c * LANES:(c + 1) * LANES]

    blocks(count, 16, 4, one)


def join_rows(src, dst, dst_row, count):
    w = dst.shape[-1] // LANES

    def one(r0):
        parts = [src[pl.ds(r0 * w + c, 16, stride=w), :] for c in range(w)]
        dst[pl.ds(pl.multiple_of(dst_row + r0, 16), 16), :] = jnp.concatenate(parts, axis=1).astype(dst.dtype)

    blocks(count, 16, 4, one)


def pick_rows(src, dst, dst_row, count, w, index):
    def body(b, carry):
        vals = []
        for u in range(UNROLL):
            line = pl.multiple_of(index(b * UNROLL + u), w)
            vals.append(src[pl.ds(line, w), :])
        for u in range(UNROLL):
            dst[pl.ds(pl.multiple_of((dst_row + b * UNROLL + u) * w, w), w), :] = vals[u]
        return carry

    lax.fori_loop(0, count // UNROLL, body, 0)


def any_spec():
    return pl.BlockSpec(memory_space=pl.ANY)


def smem_spec():
    return pl.BlockSpec(memory_space=pltpu.SMEM)


def vmem_spec():
    return pl.BlockSpec(memory_space=pltpu.VMEM)


DMA = pltpu.SemaphoreType.DMA


K0 = 0.7978845608028654
K1 = 0.044715


def dot_nn(a, b):
    return lax.dot_general(a, b, (((1,), (0,)), ((), ())), preferred_element_type=F32)


def dot_nt(a, b):
    return lax.dot_general(a, b, (((1,), (1,)), ((), ())), preferred_element_type=F32)


def gelu_pair(u, dh):
    u2 = u * u
    t = jnp.tanh(u * (K0 + (K0 * K1) * u2))
    s = 0.5 + 0.5 * t
    h = u * s
    slope = s + h * (1.0 - s) * (2.0 * K0 + (6.0 * K0 * K1) * u2)
    return h.astype(BF16), (dh * slope).astype(BF16)


def mlp_kernel(n, tc, x_hbm, g_ref, w1_ref, w2_ref, do_hbm, out_hbm, dx_hbm, dw1_hbm, dw2_hbm,
               x_v, do_v, n_v, nt_v, dot_v, y_v, dn_v, h_v, du_v, dw1_v, dw2_v, in_sem, out_sem, dw_sem):
    t_all, d = x_v.shape
    nc = t_all // tc
    rows = lambda c: pl.ds(pl.multiple_of(c * tc, tc), tc)
    for c in range(nc):
        pltpu.make_async_copy(x_hbm.at[pl.ds(c * tc, tc)], x_v.at[pl.ds(c * tc, tc)], in_sem.at[0, c]).start()
        pltpu.make_async_copy(do_hbm.at[pl.ds(c * tc, tc)], do_v.at[pl.ds(c * tc, tc)], in_sem.at[1, c]).start()
    gain = g_ref[...].astype(F32)

    def prep(c, carry):
        r = rows(c)
        pltpu.make_async_copy(x_hbm.at[r], x_v.at[r], in_sem.at[0, c]).wait()
        pltpu.make_async_copy(do_hbm.at[r], do_v.at[r], in_sem.at[1, c]).wait()
        xf = x_v[r, :].astype(F32)
        inv = lax.rsqrt(jnp.mean(xf * xf, axis=-1, keepdims=True) + EPS)
        nb = (xf * inv * gain).astype(BF16)
        n_v[r, :] = nb
        nt_v[:, r] = nb.T
        dot_v[:, r] = do_v[r, :].T
        y_v[r, :] = jnp.zeros((tc, d), F32)
        dn_v[r, :] = jnp.zeros((tc, d), F32)
        return carry

    lax.fori_loop(0, nc, prep, 0)

    def first(j, c, slot):
        r = rows(c)
        u = dot_nn(n_v[r, :], w1_ref[j]).astype(BF16).astype(F32)
        dh = dot_nt(do_v[r, :], w2_ref[j])
        h, du = gelu_pair(u, dh)
        h_v[slot] = h
        du_v[slot] = du

    def second(j, c, slot):
        r = rows(c)
        h = h_v[slot]
        du = du_v[slot]
        y_v[r, :] += dot_nn(h, w2_ref[j])
        dn_v[r, :] += dot_nt(du, w1_ref[j])
        b = lax.rem(j, 2)
        dw1_v[b] += dot_nn(nt_v[:, r], du)
        dw2_v[b] += dot_nn(dot_v[:, r], h)

    steps = n * nc
    first(0, 0, 0)

    def body(i, carry):
        j, c = lax.div(i, nc), lax.rem(i, nc)
        b = lax.rem(j, 2)

        @pl.when(c == 0)
        def _():
            @pl.when(j >= 2)
            def _():
                pltpu.make_async_copy(dw1_v.at[b], dw1_hbm.at[j - 2], dw_sem.at[0, b]).wait()
                pltpu.make_async_copy(dw2_v.at[b], dw2_hbm.at[j - 2], dw_sem.at[1, b]).wait()
            dw1_v[b] = jnp.zeros(dw1_v.shape[1:], F32)
            dw2_v[b] = jnp.zeros(dw2_v.shape[1:], F32)

        nxt = lax.rem(i + 1, steps)
        slot = lax.rem(i, 2)
        second(j, c, slot)
        first(lax.div(nxt, nc), lax.rem(nxt, nc), 1 - slot)

        @pl.when(c == nc - 1)
        def _():
            pltpu.make_async_copy(dw1_v.at[b], dw1_hbm.at[j], dw_sem.at[0, b]).start()
            pltpu.make_async_copy(dw2_v.at[b], dw2_hbm.at[j], dw_sem.at[1, b]).start()
        return carry

    lax.fori_loop(0, steps, body, 0)

    def tail(c, carry):
        r = rows(c)
        xf = x_v[r, :].astype(F32)
        inv = lax.rsqrt(jnp.mean(xf * xf, axis=-1, keepdims=True) + EPS)
        w = dn_v[r, :] * gain
        proj = jnp.mean(xf * w, axis=-1, keepdims=True) * (inv * inv * inv)
        dx = do_v[r, :].astype(F32) + (w * inv - xf * proj)
        do_v[r, :] = dx.astype(BF16)
        x_v[r, :] = (xf + y_v[r, :]).astype(BF16)
        pltpu.make_async_copy(do_v.at[r], dx_hbm.at[r], out_sem.at[1]).start()
        pltpu.make_async_copy(x_v.at[r], out_hbm.at[r], out_sem.at[0]).start()
        return carry

    lax.fori_loop(0, nc, tail, 0)
    for b in range(2):
        j = n - 2 + b
        pltpu.make_async_copy(dw1_v.at[j % 2], dw1_hbm.at[j], dw_sem.at[0, j % 2]).wait()
        pltpu.make_async_copy(dw2_v.at[j % 2], dw2_hbm.at[j], dw_sem.at[1, j % 2]).wait()
    pltpu.make_async_copy(do_v, dx_hbm, out_sem.at[1]).wait()
    pltpu.make_async_copy(x_v, out_hbm, out_sem.at[0]).wait()


def mlp(x, g, w1s, w2s, dout, tc=1024):
    t, d = x.shape
    n, _, fs = w1s.shape
    nc = t // tc
    any_ = pl.BlockSpec(memory_space=pl.ANY)
    vm = pl.BlockSpec(memory_space=pltpu.VMEM)
    return pl.pallas_call(
        functools.partial(mlp_kernel, n, tc),
        out_shape=(
            jax.ShapeDtypeStruct((t, d), BF16),
            jax.ShapeDtypeStruct((t, d), BF16),
            jax.ShapeDtypeStruct((n, d, fs), F32),
            jax.ShapeDtypeStruct((n, d, fs), F32),
        ),
        in_specs=[any_, vm, vm, vm, any_],
        out_specs=[any_] * 4,
        scratch_shapes=[
            pltpu.VMEM((t, d), BF16), pltpu.VMEM((t, d), BF16), pltpu.VMEM((t, d), BF16),
            pltpu.VMEM((d, t), BF16), pltpu.VMEM((d, t), BF16),
            pltpu.VMEM((t, d), F32), pltpu.VMEM((t, d), F32),
            pltpu.VMEM((2, tc, fs), BF16), pltpu.VMEM((2, tc, fs), BF16),
            pltpu.VMEM((2, d, fs), F32), pltpu.VMEM((2, d, fs), F32),
            pltpu.SemaphoreType.DMA((2, nc)), pltpu.SemaphoreType.DMA((2,)), pltpu.SemaphoreType.DMA((2, 2)),
        ],
        compiler_params=pltpu.CompilerParams(vmem_limit_bytes=63 << 20),
        cost_estimate=pl.CostEstimate(flops=12 * t * d * n * fs, bytes_accessed=40 << 20, transcendentals=t * n * fs),
    )(x, g.reshape(1, d), w1s, w2s, dout)


def share_kernel(n, others, pack, need, lists, most, got, relay, ss, rs, ns, nr, own_sem, xs_sem, xr_sem):
    me = lax.axis_index(AXIS)
    pl_len = pack.shape[0]
    here = pl.ds(pl.multiple_of(me * pl_len, PAGE), pl_len)
    own = pltpu.make_async_copy(pack, lists.at[here], own_sem)
    own.start()
    hops = []
    for name, size in others:
        reach = 1
        while reach < size:
            hops.append((name, size, reach))
            reach *= 2
    sem = pltpu.get_barrier_semaphore()
    for k in range(1, n):
        pl.semaphore_signal(sem, inc=1, device_id={AXIS: lax.rem(me + k, n)}, device_id_type=MESH)
    for name, size, reach in hops:
        at = lax.axis_index(name)
        pl.semaphore_signal(sem, inc=1, device_id={name: lax.rem(at + size - reach, size)}, device_id_type=MESH)
    pl.semaphore_wait(sem, n - 1 + len(hops))

    def list_copy(k):
        return pltpu.make_async_remote_copy(pack, lists.at[here], ss.at[k], rs.at[k],
                                            device_id={AXIS: lax.rem(me + k, n)}, device_id_type=MESH)

    def need_copy(k):
        return pltpu.make_async_remote_copy(need, got.at[k], ns.at[k], nr.at[k],
                                            device_id={AXIS: lax.rem(me + k, n)}, device_id_type=MESH)

    for k in far_first(n):
        need_copy(k).start()
        list_copy(k).start()
    top = need[...]
    for k in range(1, n):
        need_copy(k).wait_recv()
        top = jnp.maximum(top, got[k])
    for i, (name, size, reach) in enumerate(hops):
        relay[2 * i] = top
        at = lax.axis_index(name)
        hop = pltpu.make_async_remote_copy(relay.at[2 * i], relay.at[2 * i + 1], xs_sem.at[i], xr_sem.at[i],
                                           device_id={name: lax.rem(at + reach, size)}, device_id_type=MESH)
        hop.start()
        hop.wait()
        top = jnp.maximum(top, relay[2 * i + 1])
    most[...] = top
    for k in range(1, n):
        need_copy(k).wait_send()
        list_copy(k).wait()
    own.wait()


def share(n, others, pack, need):
    steps = max(1, sum((size - 1).bit_length() for _, size in others))
    tile = (8, LANES)
    return pl.pallas_call(
        functools.partial(share_kernel, n, others),
        out_shape=(jax.ShapeDtypeStruct((n * pack.shape[0],), I32), jax.ShapeDtypeStruct(tile, I32)),
        in_specs=[any_spec(), vmem_spec()],
        out_specs=(any_spec(), vmem_spec()),
        scratch_shapes=[pltpu.VMEM((n,) + tile, I32), pltpu.VMEM((2 * steps,) + tile, I32),
                        DMA((n,)), DMA((n,)), DMA((n,)), DMA((n,)), DMA, DMA((steps,)), DMA((steps,))],
        compiler_params=pltpu.CompilerParams(collective_id=1, has_side_effects=True),
        name='share_lists',
    )(pack, need)


def serve_kernel(n, c1, c2, rnd_ref, who_ref, ls, table, sent, e_st, ef, g, e_sem):
    me, rnd = who_ref[0], rnd_ref[0]
    vocab, d = e_st.shape
    w = d // LANES
    pl_len = ls.shape[0] // n
    head = pl_len - PAGE
    last = head - c1 - c2
    parts = e_sem.shape[0]
    step = vocab // parts

    def load(i):
        return pltpu.make_async_copy(table.at[pl.ds(i * step, step)], e_st.at[pl.ds(i * step, step)], e_sem.at[i])

    for i in range(parts):
        load(i).start()
    for i in range(parts):
        load(i).wait()
        split_rows(e_st.at[pl.ds(i * step, step)], ef, i * step, step)

    def source(q, carry):
        at1 = q * pl_len + jnp.minimum(ls[q * pl_len + head + me] + rnd * c1, last)
        at2 = q * pl_len + jnp.minimum(ls[q * pl_len + head + 16 + me] + rnd * c2, last)
        pick_rows(ef, g, 0, c1, w, lambda j: ls[at1 + j])
        pick_rows(ef, g, c1, c2, w, lambda j: ls[at2 + j])
        join_rows(g, sent.at[q], 0, c1 + c2)
        return carry

    lax.fori_loop(0, n, source, 0)


def serve(n, c1, c2, rnd, who, lists, table):
    vocab, d = table.shape
    w = d // LANES
    c = c1 + c2
    parts = 3 if vocab % 48 == 0 else 1
    return pl.pallas_call(
        functools.partial(serve_kernel, n, c1, c2),
        out_shape=jax.ShapeDtypeStruct((n, c, d), BF16),
        in_specs=[smem_spec(), smem_spec(), smem_spec(), any_spec()],
        out_specs=vmem_spec(),
        scratch_shapes=[pltpu.VMEM((vocab, d), BF16), pltpu.VMEM((vocab * w, LANES), F32),
                        pltpu.VMEM((c * w, LANES), F32), DMA((parts,))],
        compiler_params=pltpu.CompilerParams(vmem_limit_bytes=48 << 20),
        name='serve_rows',
    )(rnd, who, lists, table)


def swap_kernel(n, arrays, *refs):
    srcs, dsts, (ss, rs) = refs[:arrays], refs[arrays:2 * arrays], refs[2 * arrays:]
    me = lax.axis_index(AXIS)
    group_barrier(n, me)

    def copy(a, k):
        p = lax.rem(me + k, n)
        return pltpu.make_async_remote_copy(srcs[a].at[p], dsts[a].at[me], ss.at[a, k], rs.at[a, k],
                                            device_id={AXIS: p}, device_id_type=MESH)

    for k in far_first(n):
        for a in range(arrays):
            copy(a, k).start()
    for k in far_first(n):
        for a in range(arrays):
            copy(a, k).wait()


def swap(n, cid, name, *arrays):
    m = len(arrays)
    return pl.pallas_call(
        functools.partial(swap_kernel, n, m),
        out_shape=tuple(jax.ShapeDtypeStruct(a.shape, a.dtype) for a in arrays),
        in_specs=[any_spec()] * m,
        out_specs=(any_spec(),) * m,
        scratch_shapes=[DMA((m, n)), DMA((m, n))],
        compiler_params=pltpu.CompilerParams(collective_id=cid, has_side_effects=True),
        name=name,
    )(*arrays)


def expand_kernel(n, c, again, *refs):
    if again:
        rnd_ref, who_ref, toks, lines, sent, got, x_prev, x_out, rb, rf, xg, in_sem, x_sem = refs
    else:
        rnd_ref, who_ref, toks, lines, sent, got, x_out, rb, rf, xg, in_sem = refs
    me, rnd = who_ref[0], rnd_ref[0]
    t, d = x_out.shape
    w = d // LANES
    own = pltpu.make_async_copy(sent.at[me], rb.at[me], in_sem.at[me])
    own.start()
    if again:
        prev = pltpu.make_async_copy(x_prev, x_out, x_sem)
        prev.start()

    def load(q):
        return pltpu.make_async_copy(got.at[q], rb.at[q], in_sem.at[q])

    for k in range(n):
        @pl.when(k != me)
        def _():
            load(k).start()
    if again:
        prev.wait()
        split_rows(x_out, xg, 0, t)

    def source(q, carry):
        load(q).wait()
        split_rows(rb.at[q], rf, q * c, c)
        return carry

    lax.fori_loop(0, n, source, 0)
    low = rnd * (n * c * w)
    high = n * c * w

    def body(b, carry):
        vals, dst = [], []
        for u in range(UNROLL):
            i = b * UNROLL + u
            line = lines[i] - low
            here = (line >= 0) & (line < high)
            dst.append(pl.multiple_of(jnp.where(here, toks[i], t * w), w))
            vals.append(rf[pl.ds(pl.multiple_of(jnp.where(here, line, 0), w), w), :])
        for u in range(UNROLL):
            xg[pl.ds(dst[u], w), :] = vals[u]
        return carry

    lax.fori_loop(0, t // UNROLL, body, 0)
    join_rows(xg, x_out, 0, t)


def expand(n, rnd, who, toks, lines, sent, got, x_prev=None):
    again = x_prev is not None
    t = toks.shape[0]
    _, c, d = sent.shape
    w = d // LANES
    return pl.pallas_call(
        functools.partial(expand_kernel, n, c, again),
        out_shape=jax.ShapeDtypeStruct((t, d), BF16),
        in_specs=[smem_spec()] * 4 + [any_spec()] * (3 if again else 2),
        out_specs=vmem_spec(),
        scratch_shapes=[pltpu.VMEM((n, c, d), BF16), pltpu.VMEM((n * c * w, LANES), F32),
                        pltpu.VMEM((t * w + 8, LANES), F32), DMA((n,))] + ([DMA] if again else []),
        compiler_params=pltpu.CompilerParams(vmem_limit_bytes=48 << 20),
        name='expand_more' if again else 'expand_rows',
    )(rnd, who, toks, lines, sent, got, *((x_prev,) if again else ()))


def collect_kernel(n, c1, c2, vocab, rnd_ref, pack, toks, ids, dx_hbm, one, many, dx_v, dxf, g, col, in_sem):
    rnd = rnd_ref[0]
    t, d = dx_v.shape
    w = d // LANES
    parts = in_sem.shape[0]
    step = t // parts
    head = pack.shape[0] - PAGE
    last = head - c1 - c2

    def load(i):
        rows = pl.ds(pl.multiple_of(i * step, step), step)
        return pltpu.make_async_copy(dx_hbm.at[rows], dx_v.at[rows], in_sem.at[i])

    for i in range(parts):
        load(i).start()

    def name_rows(q, carry):
        at = jnp.minimum(pack[head + 16 + q] + rnd * c2, last)
        for j in range(c2):
            col[pl.ds(q * c2 + j, 1), :] = jnp.full((1, LANES), pack[at + j] + q * (vocab * w), I32)
        return carry

    lax.fori_loop(0, n, name_rows, 0)
    many[...] = jnp.zeros(many.shape, F32)
    names = col[:, :1]

    def sum_many(i, carry):
        load(i).wait()
        hot = jnp.where(names == ids[i] * w, 1.0, 0.0).astype(BF16)
        rows = pl.ds(pl.multiple_of(i * step, step), step)
        many[...] += lax.dot_general(hot, dx_v[rows, :], (((1,), (0,)), ((), ())), preferred_element_type=F32)
        split_rows(dx_v.at[rows], dxf, i * step, step)
        return carry

    lax.fori_loop(0, parts, sum_many, 0)

    def owner(q, carry):
        at = jnp.minimum(pack[head + q] + rnd * c1, last)
        pick_rows(dxf, g, 0, c1, w, lambda j: toks[at + j])
        join_rows(g, one.at[q], 0, c1)
        return carry

    lax.fori_loop(0, n, owner, 0)


def collect(n, c1, c2, vocab, rnd, pack, toks, ids, dx):
    t, d = dx.shape
    w = d // LANES
    parts = ids.shape[0]
    one, many = pl.pallas_call(
        functools.partial(collect_kernel, n, c1, c2, vocab),
        out_shape=(jax.ShapeDtypeStruct((n, c1, d), BF16), jax.ShapeDtypeStruct((n * c2, d), F32)),
        in_specs=[smem_spec(), smem_spec(), smem_spec(), vmem_spec(), any_spec()],
        out_specs=(vmem_spec(), vmem_spec()),
        scratch_shapes=[pltpu.VMEM((t, d), BF16), pltpu.VMEM((t * w, LANES), F32), pltpu.VMEM((c1 * w, LANES), F32),
                        pltpu.VMEM((n * c2, LANES), I32), DMA((parts,))],
        compiler_params=pltpu.CompilerParams(vmem_limit_bytes=48 << 20),
        name='collect_rows',
    )(rnd, pack, toks, ids, dx)
    return one, many.reshape(n, c2, d)


def place_kernel(n, c1, c2, again, *refs):
    if again:
        rnd_ref, who_ref, ls, one_own, many_own, one, many, _, out, acc, o_v, m_v, f_v, st, in_sem, out_sem = refs
    else:
        rnd_ref, who_ref, ls, one_own, many_own, one, many, out, acc, o_v, m_v, f_v, st, in_sem, out_sem = refs
    me, rnd = who_ref[0], rnd_ref[0]
    vocab, d = out.shape
    w = d // LANES
    pl_len = ls.shape[0] // n
    head = pl_len - PAGE

    def load(q):
        return (pltpu.make_async_copy(one.at[q], o_v.at[q], in_sem.at[0, q]),
                pltpu.make_async_copy(many.at[q], m_v.at[q], in_sem.at[1, q]))

    pltpu.make_async_copy(one_own.at[me], o_v.at[me], in_sem.at[0, me]).start()
    pltpu.make_async_copy(many_own.at[me], m_v.at[me], in_sem.at[1, me]).start()
    for k in range(n):
        @pl.when(k != me)
        def _():
            for part in load(k):
                part.start()
    blk = st.shape[1]

    def span(i):
        return pl.ds(pl.multiple_of(i * blk, blk), blk)

    def split8(src, row):
        def one8(r0):
            for k in range(w):
                acc[pl.ds((row + r0) * w + k, 8, stride=w), :] = src[pl.ds(r0, 8), pl.ds(k * LANES, LANES)]
        blocks(blk, 8, 8, one8)

    if again:
        def bring(i, carry):
            pltpu.make_async_copy(out.at[span(i)], st.at[0], out_sem.at[0]).start()
            pltpu.make_async_copy(out.at[span(i)], st.at[0], out_sem.at[0]).wait()
            split8(st.at[0], i * blk)
            return carry

        lax.fori_loop(0, vocab // blk, bring, 0)
    else:
        zero = jnp.zeros((16 * w, LANES), F32)

        def clear(r0):
            acc[pl.ds(r0 * w, 16 * w), :] = zero

        blocks(vocab, 16, 4, clear)
    dump = vocab * w

    def add(count, at, row0):
        def body(b, carry):
            lines, sums = [], []
            for u in range(UNROLL):
                j = b * UNROLL + u
                line = pl.multiple_of(jnp.where(j < count, ls[at + j], dump), w)
                lines.append(line)
                src = f_v[pl.ds(pl.multiple_of((row0 + j) * w, w), w), :]
                sums.append(acc[pl.ds(line, w), :] + src)
            for u in range(UNROLL):
                acc[pl.ds(lines[u], w), :] = sums[u]
            return carry

        lax.fori_loop(0, lax.div(count + UNROLL - 1, UNROLL), body, 0)

    def source(q, carry):
        for part in load(q):
            part.wait()
        at = q * pl_len + head
        split_rows(o_v.at[q], f_v, 0, c1)
        split_rows(m_v.at[q], f_v, c1, c2)
        b1, b2 = ls[at + me] + rnd * c1, ls[at + 16 + me] + rnd * c2
        e1, e2 = ls[at + me + 1], ls[at + 16 + me + 1]
        add(jnp.clip(e1 - b1, 0, c1), q * pl_len + b1, 0)
        add(jnp.clip(e2 - b2, 0, c2), q * pl_len + b2, c1)
        return carry

    lax.fori_loop(0, n, source, 0)

    def emit(i, carry):
        slot = lax.rem(i, 2)

        @pl.when(i >= 2)
        def _():
            pltpu.make_async_copy(st.at[slot], out.at[span(i - 2)], out_sem.at[slot]).wait()

        def one8(r0):
            for k in range(w):
                st[slot, pl.ds(r0, 8), pl.ds(k * LANES, LANES)] = acc[pl.ds((i * blk + r0) * w + k, 8, stride=w), :]

        blocks(blk, 8, 8, one8)
        pltpu.make_async_copy(st.at[slot], out.at[span(i)], out_sem.at[slot]).start()
        return carry

    total = vocab // blk
    lax.fori_loop(0, total, emit, 0)
    for i in range(max(0, total - 2), total):
        pltpu.make_async_copy(st.at[i % 2], out.at[span(i)], out_sem.at[i % 2]).wait()


def place(n, c1, c2, vocab, rnd, who, lists, one_own, many_own, one, many, prev=None):
    again = prev is not None
    d = one.shape[-1]
    w = d // LANES
    blk = next(b for b in range(1024, 0, -8) if vocab % b == 0)
    return pl.pallas_call(
        functools.partial(place_kernel, n, c1, c2, again),
        out_shape=jax.ShapeDtypeStruct((vocab, d), F32),
        in_specs=[smem_spec()] * 3 + [any_spec()] * (5 if again else 4),
        out_specs=any_spec(),
        scratch_shapes=[
            pltpu.VMEM((vocab * w + 8, LANES), F32), pltpu.VMEM((n, c1, d), BF16), pltpu.VMEM((n, c2, d), F32),
            pltpu.VMEM(((c1 + c2) * w, LANES), F32), pltpu.VMEM((2, blk, d), F32), DMA((2, n)), DMA((2,)),
        ],
        input_output_aliases={7: 0} if again else {},
        compiler_params=pltpu.CompilerParams(vmem_limit_bytes=48 << 20),
        name='place_more' if again else 'place_rows',
    )(rnd, who, lists, one_own, many_own, one, many, *((prev,) if again else ()))


def route(n, vocab, w, c1, c2, ids):
    t = ids.shape[0]
    c = c1 + c2
    s, p = lax.sort((ids, lax.iota(I32, t)), num_keys=1)
    edge = jnp.full((1,), -1, I32)
    first = s != jnp.concatenate([edge, s[:-1]])
    last = s != jnp.concatenate([s[1:], edge])
    lone = first & last
    lead = first & ~last
    lone_i, lead_i = lone.astype(I32), lead.astype(I32)
    bounds = lax.iota(I32, n + 1) * vocab
    below = s[None, :] < bounds[:, None]
    base1 = jnp.sum(jnp.where(below, lone_i[None, :], 0), axis=1)
    base2 = jnp.sum(jnp.where(below, lead_i[None, :], 0), axis=1)
    owner = n - jnp.sum(below[1:].astype(I32), axis=0)
    mine = owner[None, :] == lax.iota(I32, n)[:, None]
    start1 = jnp.sum(jnp.where(mine, base1[:n, None], 0), axis=0)
    start2 = jnp.sum(jnp.where(mine, base2[:n, None], 0), axis=0)
    r1 = jnp.cumsum(lone_i) - lone_i - start1
    r2 = jnp.cumsum(lead_i) - 1 - start2
    rnd1, rnd2 = r1 // c1, r2 // c2
    slot = jnp.where(lone, rnd1 * (n * c) + owner * c + r1 - rnd1 * c1, rnd2 * (n * c) + owner * c + c1 + r2 - rnd2 * c2)
    kind = jnp.where(lone, 0, jnp.where(lead, 1, 2)) * t + lax.iota(I32, t)
    _, line, tok = lax.sort((kind, (s - owner * vocab) * w, p * w), num_keys=1)
    n1 = base1[n]
    room = -(-(t + c1 + c2) // PAGE) * PAGE
    spare = jnp.zeros((16 - n - 1,), I32)
    heads = jnp.concatenate([base1, spare, n1 + base2, spare])
    fill = jnp.zeros((room - t,), I32)
    heads = jnp.concatenate([heads, jnp.zeros((PAGE - heads.shape[0],), I32)])
    pack = jnp.concatenate([line, fill, heads])
    lone_tok = jnp.concatenate([tok, fill])
    per1 = jnp.max(base1[1:] - base1[:-1])
    per2 = jnp.max(base2[1:] - base2[:-1])
    rounds = jnp.maximum((per1 + c1 - 1) // c1, (per2 + c2 - 1) // c2)
    return pack, lone_tok, p * w, slot * w, rounds


def solution(mesh):
    n = mesh.shape[AXIS]
    axes = tuple(mesh.axis_names)
    others = tuple((name, mesh.shape[name]) for name in axes if name != AXIS)
    tok_spec = P(axes)
    row_spec = P(axes, None)

    def local_step(token_ids, emb_shard, norm_gain, w_up_l, w_down_l, grad_out):
        vocab, d = emb_shard.shape
        t = token_ids.shape[0]
        w = d // LANES
        c1 = -(-(t * 5 // (8 * n)) // 16) * 16
        c2 = -(-(t // 128) // 16) * 16
        who = lax.axis_index(AXIS)[None].astype(I32)
        w_up = lax.all_gather(w_up_l, AXIS)
        w_down = lax.all_gather(w_down_l, AXIS)
        pack, lone_tok, toks, lines, rounds = route(n, vocab, w, c1, c2, token_ids)
        lists, most = share(n, others, pack, jnp.full((8, LANES), rounds, I32))
        rounds = most[0, 0]
        none = jnp.zeros((1,), I32)

        def rows_of(rnd):
            sent = serve(n, c1, c2, rnd, who, lists, emb_shard)
            return sent, swap(n, 2, 'swap_rows', sent)[0]

        def more_rows(carry):
            r, x_now = carry
            return r + 1, expand(n, r[None], who, toks, lines, *rows_of(r[None]), x_now)

        x = expand(n, none, who, toks, lines, *rows_of(none))
        _, x = lax.while_loop(lambda carry: carry[0] < rounds, more_rows, (jnp.ones((), I32), x))
        out, dx, dw1, dw2t = mlp(x, norm_gain, w_up, w_down, grad_out)
        dw = lax.psum_scatter(jnp.concatenate([dw1, dw2t], axis=1), AXIS, scatter_dimension=0)
        ids_c = token_ids.reshape(-1, 1, t // 8)

        def sums_of(rnd):
            one, many = collect(n, c1, c2, vocab, rnd, pack, lone_tok, ids_c, dx)
            return (one, many) + swap(n, 3, 'swap_sums', one, many)

        def more_sums(carry):
            r, now = carry
            return r + 1, place(n, c1, c2, vocab, r[None], who, lists, *sums_of(r[None]), now)

        d_emb = place(n, c1, c2, vocab, none, who, lists, *sums_of(none))
        _, d_emb = lax.while_loop(lambda carry: carry[0] < rounds, more_sums, (jnp.ones((), I32), d_emb))
        return out, d_emb, dw[:d], dw[d:].T

    return jax.shard_map(
        local_step,
        mesh=mesh,
        in_specs=(tok_spec, P(AXIS, None), P(None), P(None, AXIS), P(AXIS, None), row_spec),
        out_specs=(row_spec, row_spec, P(axes[0], AXIS), row_spec),
        check_vma=False,
    )
```

time: 1790 us -> 343 us (0.19)
  waiting for transfers between devices: 1170 us -> 1.56 us
  Pallas kernels: 0 us -> 284 us
  other arithmetic: 262 us -> 22.6 us
  matrix products: 167 us -> 0 us
  local copies, waits for them, and re-layouts: 149 us -> 16.8 us
  blocking collectives: 19 us -> 0 us
    reduce_scatter x3 -> x1, waiting for transfers between devices: 785 us -> 0.02 us  [local_step(): lax.psum_scatter(jnp.concatenate([dw1, dw2t], axis=1), AXIS, scatter_dime...]
    all_gather x3 -> x2, waiting for transfers between devices: 386 us -> 0.04 us  [the longest x1 0.02 us: local_step(): w_up = lax.all_gather(w_up_l, AXIS)]
    pallas_call x0 -> x8, Pallas kernels: none -> 284 us  [the longest x2 90.3 us: swap(): pl.pallas_call(functools.partial(swap_kernel, n, m), out_shape=tuple((jax...]
    scatter-add x1 -> x0, other arithmetic: 211 us -> none  [local_step(): jax.ops.segment_sum(dx_all.astype(jnp.float32), seg_ids, num_segments=voc...]
    dot_general x6 -> x0, matrix products: 167 us -> none  [the longest x2 55.4 us: contract_last(): lax.dot_general(left_op, right_op, (((1,), (1,)), ((), ())), preferred_el...]
    gather x1 -> x0, local copies, waits for them, and re-layouts: 136 us -> none  [local_step(): jnp.take(emb_shard, jnp.clip(rel_ids, 0, vocab_local - 1), axis=0)]
    select_n x2 -> x0, other arithmetic: 24 us -> none  [the longest x1 23.3 us: local_step(): jnp.where(is_owned[:, None], looked_up, jnp.zeros((), looked_up.dtype))]
    all_gather x1 -> x0, blocking collectives: 19 us -> none  [local_step(): ids_all = lax.all_gather(token_ids, 'tensor', tiled=True)]
  transfers between devices with their start and end apart: 6 -> 3, of which waited for: 6 -> 0; matrix products, arithmetic and copies ran while one was open for 6% -> 6% of each run, Pallas kernels for 0% -> 58%
where the time goes in v1:
time: 343 us; the launch traced here: 342 us
  Pallas kernels  284 us (83%)
  other arithmetic  22.6 us (7%)
  local copies, waits for them, and re-layouts  16.8 us (5%)
  between operations  15.4 us (4%)
    pallas_call x2, Pallas kernels, swap(): pl.pallas_call(functools.partial(swap_kernel, n, m), out_shape=tuple((jax...  90.3 us
    pallas_call x1, Pallas kernels, mlp(): pl.pallas_call(functools.partial(mlp_kernel, n, tc), out_shape=(jax.Shape...  84.4 us
    pallas_call x1, Pallas kernels, place(): pl.pallas_call(functools.partial(place_kernel, n, c1, c2, again), out_sha...  55.8 us
    pallas_call x1, Pallas kernels, expand(): pl.pallas_call(functools.partial(expand_kernel, n, c, again), out_shape=j...  18.6 us
    pallas_call x1, Pallas kernels, share(): pl.pallas_call(functools.partial(share_kernel, n, others), out_shape=(jax...  13.2 us
    pallas_call x1, Pallas kernels, serve(): pl.pallas_call(functools.partial(serve_kernel, n, c1, c2), out_shape=jax....  11.6 us
    unnamed x21, local copies, waits for them, and re-layouts  11.2 us
    pallas_call x1, Pallas kernels, collect(): pl.pallas_call(functools.partial(collect_kernel, n, c1, c2, vocab), out_s...  10.1 us
  transfers between devices with their start and end apart: 3, of which 0 were waited for; matrix products, arithmetic and copies ran while one was open for 6% of the time, Pallas kernels for 58%

profile of v1, /device:TPU:113, one launch (start us, length us, event | category | flops | bytes accessed | tf_op | source)
XLA Modules:
  0.0 342.1 jit_solution(16639166861431877306)
XLA Ops:
  7.2 0.1 all-gather.5.cloned.1.call-start
  7.2 0.7 all-gather.5.cloned.1.call-update
  8.0 0.1 all-gather.7.cloned.1.call-start
  8.0 0.7 all-gather.7.cloned.1.call-update
  8.8 0.1 reduce-scatter.2.cloned.1.call-start
  8.9 5.9 %sort.46 = (s32[4096]{0:T(1024)S(1)}, s32[4096]{0:T(1024)S(1)}) sort(s32[4096]{0:T(1024)} %param.10, s32[4096]{0:T(1024)S(1)} %iota.18), dimensions={0}, to_apply=%region_0.0 | sort | flops 49152 | bytes 65536 | tf_op jit(solution)/shard_map/sort | solution.py:634
  14.8 0.1 fusion.5
  14.8 0.1 iota_add_fusion
  15.0 0.3 select_reduce_fusion
  15.2 0.7 subtract_reduce_fusion
  16.6 0.7 subtract_reduce_fusion.1
  17.9 0.6 slice.64
  18.5 0.3 reduce-window.24
  18.8 0.1 slice.75
  18.9 0.3 reduce-window.16
  19.2 0.1 slice.72
  19.4 0.1 slice_reduce_fusion
  19.5 0.1 slice_reduce_fusion.1
  19.6 0.1 broadcast_compare_fusion
  19.8 0.1 select_reduce_fusion.2
  19.9 0.1 subtract_multiply_fusion
  20.1 6.0 %sort.47 = (s32[4096]{0:T(1024)}, s32[4096]{0:T(1024)S(1)}, s32[4096]{0:T(1024)S(1)}, s32[4096]{0:T(1024)}) sort(s32[4096]{0:T(1024)S(1)} %get-tuple-element.182, s32[4096]{0:T(1024)S(1)} %get-tuple-element.188, s32[4096]{0:T(1024)S(1)} %get-tuple-element.321.refs_2_, s32[4096]{0:T(1024)S(1)} %iota.21), dimensions={0}, to_apply=%region_10.11 | sort | flops 49152 | bytes 131072 | tf_op jit(solution)/shard_map/sort | solution.py:654
  26.0 0.6 broadcast_add_fusion
  26.7 0.1 concatenate.17.pack
  26.8 0.6 broadcast_in_dim.82.need
  27.4 13.2 %share_lists.1 = (s32[49152]{0:T(1024)S(1)}, s32[8,128]{1,0:T(8,128)}) custom-call(s32[6144]{0:T(1024)S(1)} %concatenate.17.pack, s32[8,128]{1,0:T(8,128)} %broadcast_in_dim.82.need), custom_call_target="tpu_custom_call" | custom-call | tf_op jit(solution)/shard_map/share_lists/pallas_call | solution.py:292
  40.6 11.6 %serve_rows.2.refs_0_.refs_4_ = bf16[8,352,512]{2,1,0:T(8,128)(2,1)S(1)} custom-call(s32[1]{0:T(128)} %constant.64.clone.1.rnd_ref.refs_0_, s32[1]{0:T(128)} %bitcast.3.who_ref.refs_1_, s32[49152]{0:T(1024)S(1)} %get-tuple-element.350.ls.refs_2_, bf16[6288,512]{1,0:T(8,128)(2,1)} %table.1), custom_call_target="tpu_custom_call" | custom-call | tf_op jit(solution)/shard_map/serve_rows/pallas_call | solution.py:339
  52.3 1.6 copy-done.7
  53.9 35.3 %swap_rows.2.refs_5_ = bf16[8,352,512]{2,1,0:T(8,128)(2,1)} custom-call(bf16[8,352,512]{2,1,0:T(8,128)(2,1)} %copy-done.7), custom_call_target="tpu_custom_call" | custom-call | tf_op jit(solution)/shard_map/swap_rows/pallas_call | solution.py:371
  89.1 1.2 slice.67
  90.3 0.6 reshape.68.g_ref
  90.9 1.8 copy-done.8
  92.7 1.8 copy-done.10
  94.5 18.6 %expand_rows.1 = bf16[4096,512]{1,0:T(8,128)(2,1)} custom-call(s32[1]{0:T(128)} %constant.64.clone.1.rnd_ref.refs_0_, s32[1]{0:T(128)} %bitcast.3.who_ref.refs_1_, s32[4096]{0:T(1024)S(1)} %get-tuple-element.321.refs_2_, s32[4096]{0:T(1024)S(1)} %get-tuple-element.322.refs_3_, bf16[8,352,512]{2,1,0:T(8,128)(2,1)S(1)} %copy-done.8, ...), custom_call_target="tpu_custom_call" | custom-call | tf_op jit(solution)/shard_map/expand_rows/pallas_call | solution.py:437
  113.2 0.8 while.20
  114.1 84.4 %shard_map.93 = (bf16[4096,512]{1,0:T(8,128)(2,1)}, bf16[4096,512]{1,0:T(8,128)(2,1)}, f32[8,512,256]{2,1,0:T(8,128)}, f32[8,512,256]{2,1,0:T(8,128)}) custom-call(bf16[4096,512]{1,0:T(8,128)(2,1)} %get-tuple-element.121.x_hbm, bf16[1,512]{1,0:T(2,128)(2,1)} %reshape.68.g_ref, bf16[8,512,256]{2,1,0:T(8,128)(2,1)} %bitcast.42, bf16[8,256,512]{2,1,0:T(8,128)(2,1)} %bitcast.43, ...), custom_call_target="tpu_custom_call" | custom-call | flops 51539607552 | bytes 41943040 | tf_op jit(solution)/shard_map/pallas_call | solution.py:216
  198.5 7.2 %pad_maximum_fusion = f32[8,1024,256]{2,1,0:T(8,128)} fusion(f32[8,512,256]{2,1,0:T(8,128)} %get-tuple-element.131, f32[8,512,256]{2,1,0:T(8,128)} %get-tuple-element.130), kind=kLoop, calls=%fused_computation | loop fusion | flops 2097152 | bytes 16777216 | tf_op jit(solution)/shard_map/concatenate | solution.py:701
  205.8 0.6 copy-done.16
  206.5 10.1 %collect_rows.2 = (bf16[8,320,512]{2,1,0:T(8,128)(2,1)S(1)}, f32[256,512]{1,0:T(8,128)S(1)}) custom-call(s32[1]{0:T(128)} %constant.64.clone.1.rnd_ref.refs_0_, s32[6144]{0:T(1024)S(1)} %concatenate.17.pack, s32[5120]{0:T(1024)S(1)} %concatenate.18.toks, s32[8,1,512]{2,1,0:T(1,128)S(1)} %bitcast.40, bf16[4096,512]{1,0:T(8,128)(2,1)} %get-tuple-element.348.dx_hbm), custom_call_target="tpu_custom_call" | custom-call | tf_op jit(solution)/shard_map/collect_rows/pallas_call | solution.py:498
  216.6 1.5 copy-done.11
  218.1 0.8 copy-done.13
  218.9 55.1 %swap_sums.2 = (bf16[8,320,512]{2,1,0:T(8,128)(2,1)}, f32[8,32,512]{2,1,0:T(8,128)}) custom-call(bf16[8,320,512]{2,1,0:T(8,128)(2,1)} %copy-done.11, f32[8,32,512]{2,1,0:T(8,128)} %bitcast.38), custom_call_target="tpu_custom_call" | custom-call | tf_op jit(solution)/shard_map/swap_sums/pallas_call | solution.py:371
  274.0 1.0 copy-done.14
  275.0 1.0 copy-done.15
  276.0 55.8 %place_rows.1 = f32[6288,512]{1,0:T(8,128)} custom-call(s32[1]{0:T(128)} %constant.64.clone.1.rnd_ref.refs_0_, s32[1]{0:T(128)} %bitcast.3.who_ref.refs_1_, s32[49152]{0:T(1024)S(1)} %get-tuple-element.377, bf16[8,320,512]{2,1,0:T(8,128)(2,1)S(1)} %copy-done.12, f32[8,32,512]{2,1,0:T(8,128)S(1)} %bitcast.39, ...), custom_call_target="tpu_custom_call" | custom-call | tf_op jit(solution)/shard_map/place_rows/pallas_call | solution.py:616
  331.9 0.7 while.21
  332.5 2.1 slice_bitcast_fusion
  334.6 1.0 copy.13
  (29 shorter events, 0.3 us)
Async XLA Ops:
  7.2 106.9 %all-gather.5.cloned.1.call-start = ((), (), s32[]{:S(2)}) async-start(), calls=%async_computation.2 | async-start | bytes 2359296 | tf_op jit(solution)/shard_map/all_gather | solution.py:683
  8.0 106.1 %all-gather.7.cloned.1.call-start = ((), (), s32[]{:S(2)}) async-start(), calls=%async_computation.3 | async-start | bytes 2359296 | tf_op jit(solution)/shard_map/all_gather | solution.py:684
  8.8 323.8 %reduce-scatter.2.cloned.1.call-start = ((), (), s32[]{:S(2)}) async-start(), calls=%async_computation.1 | async-start | bytes 9437184 | tf_op jit(solution)/shard_map/reduce_scatter | solution.py:701
  52.3 1.6 copy-start.7
  53.8 36.5 %copy-start.17 = (bf16[512]{0:T(512)(128)(2,1)S(1)}, bf16[512]{0:T(512)(128)(2,1)}, u32[]{:S(2)}) copy-start(bf16[512]{0:T(512)(128)(2,1)} %param.12) | copy-start | bytes 3076
  90.9 1.8 copy-start.8
  92.7 1.8 copy-start.10
  205.7 0.7 copy-start.16
  216.6 1.5 copy-start.11
  218.1 0.8 copy-start.13
  218.9 55.1 %copy-start.12 = (bf16[8,320,512]{2,1,0:T(8,128)(2,1)S(1)}, bf16[8,320,512]{2,1,0:T(8,128)(2,1)}, u32[]{:S(2)}) copy-start(bf16[8,320,512]{2,1,0:T(8,128)(2,1)} %copy-done.11) | copy-start | bytes 7864324
  273.9 1.0 copy-start.14
  275.0 1.0 copy-start.15
Sparse Core Ops, SparseCore 0:
  9.6 24.6 all-gather.4
  35.9 21.5 all-gather.6
  205.9 80.2 reduce-scatter.1

commit v2 on v1

v2 whole, which is shorter than its diff:
```python
import functools

import jax
import jax.numpy as jnp
from jax import lax
from jax.experimental import pallas as pl
from jax.experimental.pallas import tpu as pltpu
from jax.sharding import PartitionSpec as P

EPS = 1e-6
F32 = jnp.float32
BF16 = jnp.bfloat16
I32 = jnp.int32
MESH = pl.DeviceIdType.MESH
LANES = 128
UNROLL = 16
PAGE = 1024
AXIS = 'tensor'


def group_barrier(n, me, wait=True):
    sem = pltpu.get_barrier_semaphore()
    for k in range(1, n):
        pl.semaphore_signal(sem, inc=1, device_id={AXIS: lax.rem(me + k, n)}, device_id_type=MESH)
    if wait:
        pl.semaphore_wait(sem, n - 1)


def far_first(n):
    return sorted(range(1, n), key=lambda k: -min(k // 2, (n - k) // 2))


def blocks(count, size, many, one):
    total = count // size

    def body(b, carry):
        for u in range(many):
            one(pl.multiple_of((b * many + u) * size, size))
        return carry

    lax.fori_loop(0, total // many, body, 0)
    for b in range(total // many * many, total):
        one(b * size)


def split_rows(src, dst, dst_row, count):
    w = src.shape[-1] // LANES

    def one(r0):
        tile = src[pl.ds(r0, 16), :].astype(F32)
        for c in range(w):
            dst[pl.ds((dst_row + r0) * w + c, 16, stride=w), :] = tile[:, c * LANES:(c + 1) * LANES]

    blocks(count, 16, 4, one)


def join_rows(src, dst, dst_row, count):
    w = dst.shape[-1] // LANES

    def one(r0):
        parts = [src[pl.ds(r0 * w + c, 16, stride=w), :] for c in range(w)]
        dst[pl.ds(pl.multiple_of(dst_row + r0, 16), 16), :] = jnp.concatenate(parts, axis=1).astype(dst.dtype)

    blocks(count, 16, 4, one)


def pick_rows(src, dst, dst_row, count, w, index):
    def body(b, carry):
        vals = []
        for u in range(UNROLL):
            line = pl.multiple_of(index(b * UNROLL + u), w)
            vals.append(src[pl.ds(line, w), :])
        for u in range(UNROLL):
            dst[pl.ds(pl.multiple_of((dst_row + b * UNROLL + u) * w, w), w), :] = vals[u]
        return carry

    lax.fori_loop(0, count // UNROLL, body, 0)


def any_spec():
    return pl.BlockSpec(memory_space=pltpu.HBM)


def smem_spec():
    return pl.BlockSpec(memory_space=pltpu.SMEM)


def vmem_spec():
    return pl.BlockSpec(memory_space=pltpu.VMEM)


DMA = pltpu.SemaphoreType.DMA


K0 = 0.7978845608028654
K1 = 0.044715


def dot_nn(a, b):
    return lax.dot_general(a, b, (((1,), (0,)), ((), ())), preferred_element_type=F32)


def dot_nt(a, b):
    return lax.dot_general(a, b, (((1,), (1,)), ((), ())), preferred_element_type=F32)


def gelu_pair(u, dh):
    u2 = u * u
    t = jnp.tanh(u * (K0 + (K0 * K1) * u2))
    s = 0.5 + 0.5 * t
    h = u * s
    slope = s + h * (1.0 - s) * (2.0 * K0 + (6.0 * K0 * K1) * u2)
    return h.astype(BF16), (dh * slope).astype(BF16)


def mlp_kernel(n, tc, x_hbm, g_ref, w1_hbm, w2_hbm, do_hbm, dh_hbm, dot_hbm, out_hbm, dx_hbm, dw1_hbm, dw2_hbm,
               x_v, do_v, n_v, nt_v, dot_v, y_v, dn_v, w1_ref, w2_ref, h_a, h_b, du_a, du_b, dh_a, dh_b, part, mate, ours, theirs,
               in_sem, w_sem, dh_sem, out_sem, dw_sem, ms, mr, cs, cr):
    me = lax.axis_index(AXIS)
    core, chip = lax.rem(me, 2), lax.div(me, 2)
    chips = n // 2
    far = sorted(range(1, chips), key=lambda k: -min(k, chips - k)) + [0]
    t_all, d = x_v.shape
    nc = t_all // tc
    rows = lambda c: pl.ds(pl.multiple_of(c * tc, tc), tc)
    mate_id = {AXIS: me + 1 - 2 * core}

    def load(c):
        r = rows(c)
        return pltpu.make_async_copy(x_hbm.at[r], x_v.at[r], in_sem.at[c])

    for c in range(nc):
        load(c).start()
    weights = (pltpu.make_async_copy(w1_hbm, w1_ref, w_sem.at[0]), pltpu.make_async_copy(w2_hbm, w2_ref, w_sem.at[1]),
               pltpu.make_async_copy(dot_hbm, dot_v, w_sem.at[2]))
    for cp in weights:
        cp.start()
    group_barrier(n, me, wait=False)
    late = pltpu.make_async_copy(do_hbm, do_v, w_sem.at[3])
    late.start()

    def owner_chip(q):
        off = sum(jnp.where(q == i, k, 0) for i, k in enumerate(far))
        return lax.rem(chip + off, chips)

    def block_of(jj):
        half = lax.rem(jj, 2)
        return 2 * owner_chip(lax.div(jj, 2)) + jnp.where(half == 0, 1 - core, core)

    def mate_copy(q):
        return pltpu.make_async_remote_copy(part.at[0], mate.at[q], ms.at[q], mr.at[q],
                                            device_id=mate_id, device_id_type=MESH)

    def chip_copy(q):
        return pltpu.make_async_remote_copy(ours.at[q], theirs.at[q], cs.at[q], cr.at[q],
                                            device_id={AXIS: 2 * owner_chip(q) + core}, device_id_type=MESH)

    gain = g_ref[...].astype(F32)

    def prep(c, carry):
        r = rows(c)
        load(c).wait()
        xf = x_v[r, :].astype(F32)
        inv = lax.rsqrt(jnp.mean(xf * xf, axis=-1, keepdims=True) + EPS)
        nb = (xf * inv * gain).astype(BF16)
        n_v[r, :] = nb
        nt_v[:, r] = nb.T
        y_v[r, :] = jnp.zeros((tc, d), F32)
        dn_v[r, :] = jnp.zeros((tc, d), F32)
        return carry

    hs, dus, dhs = (h_a, h_b), (du_a, du_b), (dh_a, dh_b)

    def pull(i, slot):
        j, c = block_of(lax.div(i, nc)), lax.rem(i, nc)
        return pltpu.make_async_copy(dh_hbm.at[j, rows(c)], dhs[slot], dh_sem.at[slot])

    for i in range(2):
        pull(i, i).start()
    lax.fori_loop(0, nc, prep, 0)
    for cp in weights:
        cp.wait()
    pl.semaphore_wait(pltpu.get_barrier_semaphore(), n - 1)

    steps = n * nc
    sub = tc // 4

    def first_piece(i, slot, k):
        j, c = block_of(lax.div(i, nc)), lax.rem(i, nc)
        here = pl.ds(k * sub, sub)
        u = dot_nn(n_v[pl.ds(pl.multiple_of(c * tc + k * sub, sub), sub), :], w1_ref[j]).astype(BF16).astype(F32)
        hs[slot][here, :], dus[slot][here, :] = gelu_pair(u, dhs[slot][here, :])

    def second_piece(i, slot, k):
        jj, c = lax.div(i, nc), lax.rem(i, nc)
        j, half = block_of(jj), lax.rem(jj, 2)
        r = rows(c)
        if k == 0:
            y_v[r, :] += dot_nn(hs[slot][...], w2_ref[j])
        elif k == 1:
            dn_v[r, :] += dot_nt(dus[slot][...], w1_ref[j])
        elif k == 2:
            part[half, 0] += dot_nn(nt_v[:, r], dus[slot][...])
        else:
            part[half, 1] += dot_nn(dot_v[:, r], hs[slot][...])

    def both(i, slot):
        pull(i + 1, 1 - slot).wait()
        for k in range(4):
            first_piece(i + 1, 1 - slot, k)
            second_piece(i, slot, k)

        @pl.when(i + 3 < steps)
        def _():
            pull(i + 3, 1 - slot).start()

    def opens(i):
        jj = lax.div(i, nc)
        q, half = lax.div(jj, 2), lax.rem(jj, 2)

        @pl.when(lax.rem(i, nc) == 0)
        def _():
            @pl.when((half == 0) & (q >= 1))
            def _():
                mate_copy(q - 1).wait_send()

            part[half] = jnp.zeros(part.shape[1:], F32)

    def closes(i):
        jj = lax.div(i, nc)
        q, half = lax.div(jj, 2), lax.rem(jj, 2)

        @pl.when((lax.rem(i, nc) == nc - 1) & (half == 0))
        def _():
            mate_copy(q).start()

        @pl.when((lax.rem(i, nc) == nc - 1) & (half == 1))
        def _():
            mate_copy(q).wait_recv()
            ours[q] = part[1] + mate[q]
            chip_copy(q).start()

    pull(0, 0).wait()
    for k in range(4):
        first_piece(0, 0, k)
    pull(2, 0).start()

    def body(m, carry):
        i = 2 * m
        opens(i)
        both(i, 0)
        both(i + 1, 1)
        closes(i + 1)
        return carry

    lax.fori_loop(0, steps // 2 - 1, body, 0)
    opens(steps - 2)
    both(steps - 2, 0)
    for k in range(4):
        second_piece(steps - 1, 1, k)
    mate_copy(chips - 1).wait_recv()
    late.wait()

    def tail(c, carry):
        r = rows(c)
        xf = x_v[r, :].astype(F32)
        inv = lax.rsqrt(jnp.mean(xf * xf, axis=-1, keepdims=True) + EPS)
        w = dn_v[r, :] * gain
        proj = jnp.mean(xf * w, axis=-1, keepdims=True) * (inv * inv * inv)
        dx = do_v[r, :].astype(F32) + (w * inv - xf * proj)
        do_v[r, :] = dx.astype(BF16)
        x_v[r, :] = (xf + y_v[r, :]).astype(BF16)
        pltpu.make_async_copy(do_v.at[r], dx_hbm.at[r], out_sem.at[1]).start()
        pltpu.make_async_copy(x_v.at[r], out_hbm.at[r], out_sem.at[0]).start()
        return carry

    lax.fori_loop(0, nc, tail, 0)
    total = part[1] + mate[chips - 1]
    for q in range(chips - 1):
        chip_copy(q).wait_recv()
        total = total + theirs[q]
    part[1] = total
    up = pltpu.make_async_copy(part.at[1, 0], dw1_hbm, dw_sem.at[0])
    down = pltpu.make_async_copy(part.at[1, 1], dw2_hbm, dw_sem.at[1])
    up.start()
    down.start()
    mate_copy(chips - 1).wait_send()
    for q in range(chips - 1):
        chip_copy(q).wait_send()
    up.wait()
    down.wait()
    pltpu.make_async_copy(do_v, dx_hbm, out_sem.at[1]).wait()
    pltpu.make_async_copy(x_v, out_hbm, out_sem.at[0]).wait()


def mlp(n, cid, x, g, w1s, w2s, dout, dh, dot, tc=1024):
    t, d = x.shape
    fs = w1s.shape[2]
    nc = t // tc
    chips = n // 2
    return pl.pallas_call(
        functools.partial(mlp_kernel, n, tc),
        out_shape=(
            jax.ShapeDtypeStruct((t, d), BF16),
            jax.ShapeDtypeStruct((t, d), BF16),
            jax.ShapeDtypeStruct((d, fs), F32),
            jax.ShapeDtypeStruct((d, fs), F32),
        ),
        in_specs=[any_spec(), vmem_spec()] + [any_spec()] * 5,
        out_specs=(any_spec(),) * 4,
        scratch_shapes=[
            pltpu.VMEM((t, d), BF16), pltpu.VMEM((t, d), BF16), pltpu.VMEM((t, d), BF16),
            pltpu.VMEM((d, t), BF16), pltpu.VMEM((d, t), BF16),
            pltpu.VMEM((t, d), F32), pltpu.VMEM((t, d), F32),
            pltpu.VMEM(w1s.shape, BF16), pltpu.VMEM(w2s.shape, BF16),
            pltpu.VMEM((tc, fs), BF16), pltpu.VMEM((tc, fs), BF16), pltpu.VMEM((tc, fs), BF16), pltpu.VMEM((tc, fs), BF16),
            pltpu.VMEM((tc, fs), F32), pltpu.VMEM((tc, fs), F32),
            pltpu.VMEM((2, 2, d, fs), F32), pltpu.VMEM((chips, 2, d, fs), F32),
            pltpu.VMEM((chips - 1, 2, d, fs), F32), pltpu.VMEM((chips - 1, 2, d, fs), F32),
            DMA((nc,)), DMA((4,)), DMA((2,)), DMA((2,)), DMA((2,)), DMA((chips,)), DMA((chips,)), DMA((chips,)), DMA((chips,)),
        ],
        compiler_params=pltpu.CompilerParams(
            collective_id=cid, has_side_effects=True, vmem_limit_bytes=63 << 20),
        cost_estimate=pl.CostEstimate(flops=12 * t * d * n * fs, bytes_accessed=40 << 20, transcendentals=t * n * fs),
        name='mlp_block',
    )(x, g.reshape(1, d), w1s, w2s, dout, dh, dot)


def share_kernel(n, pack, lists, ss, rs, own_sem):
    me = lax.axis_index(AXIS)
    pl_len = pack.shape[0]
    here = pl.ds(pl.multiple_of(me * pl_len, PAGE), pl_len)
    own = pltpu.make_async_copy(pack, lists.at[here], own_sem)
    own.start()
    group_barrier(n, me)

    def list_copy(k):
        return pltpu.make_async_remote_copy(pack, lists.at[here], ss.at[k], rs.at[k],
                                            device_id={AXIS: lax.rem(me + k, n)}, device_id_type=MESH)

    for k in far_first(n):
        list_copy(k).start()
    for k in far_first(n):
        list_copy(k).wait()
    own.wait()


def share(n, pack):
    return pl.pallas_call(
        functools.partial(share_kernel, n),
        out_shape=jax.ShapeDtypeStruct((n * pack.shape[0],), I32),
        in_specs=[any_spec()],
        out_specs=any_spec(),
        scratch_shapes=[DMA((n,)), DMA((n,)), DMA],
        compiler_params=pltpu.CompilerParams(collective_id=1, has_side_effects=True, vmem_limit_bytes=63 << 20),
        name='share_lists',
    )(pack)


def serve_kernel(n, c1, c2, rnd_ref, who_ref, lists, table, out, ls, e_st, ef, g, sent, l_sem, e_sem, o_sem):
    me, rnd = who_ref[0], rnd_ref[0]
    vocab, d = e_st.shape
    w = d // LANES
    asked = pltpu.make_async_copy(lists, ls, l_sem)
    asked.start()
    pl_len = ls.shape[0] // n
    head = pl_len - PAGE
    last = head - c1 - c2
    parts = e_sem.shape[0]
    step = vocab // parts

    def load(i):
        return pltpu.make_async_copy(table.at[pl.ds(i * step, step)], e_st.at[pl.ds(i * step, step)], e_sem.at[i])

    for i in range(parts):
        load(i).start()
    for i in range(parts):
        load(i).wait()
        split_rows(e_st.at[pl.ds(i * step, step)], ef, i * step, step)

    asked.wait()

    def source(q, carry):
        at1 = q * pl_len + jnp.minimum(ls[q * pl_len + head + me] + rnd * c1, last)
        at2 = q * pl_len + jnp.minimum(ls[q * pl_len + head + 16 + me] + rnd * c2, last)
        pick_rows(ef, g, 0, c1, w, lambda j: ls[at1 + j])
        pick_rows(ef, g, c1, c2, w, lambda j: ls[at2 + j])
        join_rows(g, sent.at[q], 0, c1 + c2)
        pltpu.make_async_copy(sent.at[q], out.at[q], o_sem).start()
        return carry

    lax.fori_loop(0, n, source, 0)
    pltpu.make_async_copy(sent, out, o_sem).wait()


def serve(n, c1, c2, rnd, who, lists, table):
    vocab, d = table.shape
    w = d // LANES
    c = c1 + c2
    parts = 3 if vocab % 48 == 0 else 1
    return pl.pallas_call(
        functools.partial(serve_kernel, n, c1, c2),
        out_shape=jax.ShapeDtypeStruct((n, c, d), BF16),
        in_specs=[smem_spec(), smem_spec(), any_spec(), any_spec()],
        out_specs=any_spec(),
        scratch_shapes=[pltpu.SMEM(lists.shape, I32), pltpu.VMEM((vocab, d), BF16), pltpu.VMEM((vocab * w, LANES), F32),
                        pltpu.VMEM((c * w, LANES), F32), pltpu.VMEM((n, c, d), BF16), DMA, DMA((parts,)), DMA],
        compiler_params=pltpu.CompilerParams(vmem_limit_bytes=63 << 20),
        name='serve_rows',
    )(rnd, who, lists, table)


def swap_kernel(n, arrays, *refs):
    srcs, dsts, (ss, rs) = refs[:arrays], refs[arrays:2 * arrays], refs[2 * arrays:]
    me = lax.axis_index(AXIS)
    group_barrier(n, me)

    def copy(a, k):
        p = lax.rem(me + k, n)
        return pltpu.make_async_remote_copy(srcs[a].at[p], dsts[a].at[me], ss.at[a, k], rs.at[a, k],
                                            device_id={AXIS: p}, device_id_type=MESH)

    for k in far_first(n):
        for a in range(arrays):
            copy(a, k).start()
    for k in far_first(n):
        for a in range(arrays):
            copy(a, k).wait()


def swap(n, cid, name, *arrays):
    m = len(arrays)
    return pl.pallas_call(
        functools.partial(swap_kernel, n, m),
        out_shape=tuple(jax.ShapeDtypeStruct(a.shape, a.dtype) for a in arrays),
        in_specs=[any_spec()] * m,
        out_specs=(any_spec(),) * m,
        scratch_shapes=[DMA((m, n)), DMA((m, n))],
        compiler_params=pltpu.CompilerParams(collective_id=cid, has_side_effects=True, vmem_limit_bytes=63 << 20),
        name=name,
    )(*arrays)


def swap_first_kernel(n, others, tc, sent, need, do_hbm, w2_hbm, got, most, dh_hbm, dot_hbm, do_v, w2_v, dot_v, dh_v,
                      peers, relay, ss, rs, ns, nr, xs_sem, xr_sem, in_sem, w_sem, dh_sem, dot_sem):
    me = lax.axis_index(AXIS)
    t, d = do_v.shape
    nc = t // tc
    rows = lambda c: pl.ds(pl.multiple_of(c * tc, tc), tc)
    hops = []
    for name, size in others:
        reach = 1
        while reach < size:
            hops.append((name, size, reach))
            reach *= 2

    def load(c):
        return pltpu.make_async_copy(do_hbm.at[rows(c)], do_v.at[rows(c)], in_sem.at[c])

    weights = pltpu.make_async_copy(w2_hbm, w2_v, w_sem)
    weights.start()
    for c in range(nc):
        load(c).start()
    sem = pltpu.get_barrier_semaphore()
    for k in range(1, n):
        pl.semaphore_signal(sem, inc=1, device_id={AXIS: lax.rem(me + k, n)}, device_id_type=MESH)
    for name, size, reach in hops:
        at = lax.axis_index(name)
        pl.semaphore_signal(sem, inc=1, device_id={name: lax.rem(at + size - reach, size)}, device_id_type=MESH)
    pl.semaphore_wait(sem, n - 1 + len(hops))

    def row_copy(k):
        p = lax.rem(me + k, n)
        return pltpu.make_async_remote_copy(sent.at[p], got.at[me], ss.at[k], rs.at[k],
                                            device_id={AXIS: p}, device_id_type=MESH)

    def need_copy(k):
        return pltpu.make_async_remote_copy(need, peers.at[k], ns.at[k], nr.at[k],
                                            device_id={AXIS: lax.rem(me + k, n)}, device_id_type=MESH)

    for k in far_first(n):
        need_copy(k).start()
    for k in far_first(n):
        row_copy(k).start()
    weights.wait()

    def put(i):
        return pltpu.make_async_copy(dh_v.at[lax.rem(i, 2)], dh_hbm.at[lax.rem(i, n), rows(lax.div(i, n))],
                                     dh_sem.at[lax.rem(i, 2)])

    def body(i, carry):
        c, j = lax.div(i, n), lax.rem(i, n)

        @pl.when(j == 0)
        def _():
            load(c).wait()
            dot_v[:, rows(c)] = do_v[rows(c), :].T

        @pl.when(i >= 2)
        def _():
            put(i - 2).wait()

        dh_v[lax.rem(i, 2)] = dot_nt(do_v[rows(c), :], w2_v[j])
        put(i).start()
        return carry

    steps = n * nc
    lax.fori_loop(0, steps, body, 0)
    turned = pltpu.make_async_copy(dot_v, dot_hbm, dot_sem)
    turned.start()
    top = need[...]
    for k in range(1, n):
        need_copy(k).wait_recv()
        top = jnp.maximum(top, peers[k])
    for i, (name, size, reach) in enumerate(hops):
        relay[2 * i] = top
        at = lax.axis_index(name)
        hop = pltpu.make_async_remote_copy(relay.at[2 * i], relay.at[2 * i + 1], xs_sem.at[i], xr_sem.at[i],
                                           device_id={name: lax.rem(at + reach, size)}, device_id_type=MESH)
        hop.start()
        hop.wait()
        top = jnp.maximum(top, relay[2 * i + 1])
    most[...] = top
    for i in range(steps - 2, steps):
        put(i).wait()
    turned.wait()
    for k in far_first(n):
        need_copy(k).wait_send()
        row_copy(k).wait()


def swap_first(n, others, sent, need, dout, w2s, tc=1024):
    t, d = dout.shape
    fs = w2s.shape[1]
    nc = t // tc
    hops = max(1, sum((size - 1).bit_length() for _, size in others))
    tile = (8, LANES)
    return pl.pallas_call(
        functools.partial(swap_first_kernel, n, others, tc),
        out_shape=(jax.ShapeDtypeStruct(sent.shape, sent.dtype), jax.ShapeDtypeStruct(tile, I32),
                   jax.ShapeDtypeStruct((n, t, fs), F32), jax.ShapeDtypeStruct((d, t), BF16)),
        in_specs=[any_spec(), vmem_spec(), any_spec(), any_spec()],
        out_specs=(any_spec(), vmem_spec(), any_spec(), any_spec()),
        scratch_shapes=[
            pltpu.VMEM((t, d), BF16), pltpu.VMEM(w2s.shape, BF16), pltpu.VMEM((d, t), BF16), pltpu.VMEM((2, tc, fs), F32),
            pltpu.VMEM((n,) + tile, I32), pltpu.VMEM((2 * hops,) + tile, I32),
            DMA((n,)), DMA((n,)), DMA((n,)), DMA((n,)), DMA((hops,)), DMA((hops,)), DMA((nc,)), DMA, DMA((2,)), DMA,
        ],
        compiler_params=pltpu.CompilerParams(collective_id=5, has_side_effects=True, vmem_limit_bytes=63 << 20),
        name='swap_first',
    )(sent, need, dout, w2s)


def expand_kernel(n, c, again, *refs):
    if again:
        who_ref, toks_h, lines_h, sent, got, x_prev, out, toks, lines, rb, rf, xg, x_out, i_sem, in_sem, o_sem, x_sem = refs
    else:
        who_ref, toks_h, lines_h, sent, got, out, toks, lines, rb, rf, xg, x_out, i_sem, in_sem, o_sem = refs
    me = who_ref[0]
    t, d = x_out.shape
    w = d // LANES
    idx = (pltpu.make_async_copy(toks_h, toks, i_sem.at[0]), pltpu.make_async_copy(lines_h, lines, i_sem.at[1]))
    for cp in idx:
        cp.start()
    own = pltpu.make_async_copy(sent.at[me], rb.at[me], in_sem.at[me])
    own.start()
    if again:
        prev = pltpu.make_async_copy(x_prev, x_out, x_sem)
        prev.start()

    def load(q):
        return pltpu.make_async_copy(got.at[q], rb.at[q], in_sem.at[q])

    for k in range(n):
        @pl.when(k != me)
        def _():
            load(k).start()
    if again:
        prev.wait()
        split_rows(x_out, xg, 0, t)

    def source(q, carry):
        load(q).wait()
        split_rows(rb.at[q], rf, q * c, c)
        return carry

    lax.fori_loop(0, n, source, 0)

    for cp in idx:
        cp.wait()

    def body(b, carry):
        vals = [rf[pl.ds(pl.multiple_of(lines[b * UNROLL + u], w), w), :] for u in range(UNROLL)]
        for u in range(UNROLL):
            xg[pl.ds(pl.multiple_of(toks[b * UNROLL + u], w), w), :] = vals[u]
        return carry

    lax.fori_loop(0, t // UNROLL, body, 0)
    step = t // 4
    for i in range(4):
        join_rows(xg.at[pl.ds(i * step * w, step * w)], x_out, i * step, step)
        part = pl.ds(i * step, step)
        pltpu.make_async_copy(x_out.at[part], out.at[part], o_sem).start()
    pltpu.make_async_copy(x_out, out, o_sem).wait()


def expand(n, rnd, who, toks, lines, sent, got, x_prev=None):
    again = x_prev is not None
    t = toks.shape[0]
    _, c, d = sent.shape
    w = d // LANES
    lines = lines - rnd[0] * (n * c * w)
    here = (lines >= 0) & (lines < n * c * w)
    toks, lines = jnp.where(here, toks, t * w), jnp.where(here, lines, 0)
    return pl.pallas_call(
        functools.partial(expand_kernel, n, c, again),
        out_shape=jax.ShapeDtypeStruct((t, d), BF16),
        in_specs=[smem_spec()] + [any_spec()] * (5 if again else 4),
        out_specs=any_spec(),
        scratch_shapes=[pltpu.SMEM((t,), I32), pltpu.SMEM((t,), I32),
                        pltpu.VMEM((n, c, d), BF16), pltpu.VMEM((n * c * w, LANES), F32),
                        pltpu.VMEM((t * w + 8, LANES), F32), pltpu.VMEM((t, d), BF16), DMA((2,)), DMA((n,)), DMA] + ([DMA] if again else []),
        compiler_params=pltpu.CompilerParams(vmem_limit_bytes=63 << 20),
        name='expand_more' if again else 'expand_rows',
    )(who, toks, lines, sent, got, *((x_prev,) if again else ()))


def collect_kernel(n, c1, c2, vocab, again, *refs):
    if again:
        rnd_ref, pack_h, toks_h, ids, dx_hbm, one_out, many_out, *rest = refs
    else:
        rnd_ref, pack_h, toks_h, ids, dx_hbm, y_in, up_in, down_in, one_out, many_out, y_out, up_out, down_out, *rest = refs
        *rest, y_v, up_v, down_v, side_v, side_sem = rest
    pack, toks, dx_v, dxf, g, col, one, many, i_sem, in_sem, o_sem = rest
    rnd = rnd_ref[0]
    t, d = dx_v.shape
    w = d // LANES
    parts = in_sem.shape[0]
    step = t // parts
    head = pack.shape[0] - PAGE
    last = head - c1 - c2

    def load(i):
        rows = pl.ds(pl.multiple_of(i * step, step), step)
        return pltpu.make_async_copy(dx_hbm.at[rows], dx_v.at[rows], in_sem.at[i])

    idx = (pltpu.make_async_copy(pack_h, pack, i_sem.at[0]), pltpu.make_async_copy(toks_h, toks, i_sem.at[1]))
    for cp in idx:
        cp.start()
    for i in range(parts):
        load(i).start()
    if not again:
        side_in = (pltpu.make_async_copy(y_in, y_v, side_sem.at[0]), pltpu.make_async_copy(up_in, up_v, side_sem.at[1]),
                   pltpu.make_async_copy(down_in, down_v, side_sem.at[2]))
        side_out = (pltpu.make_async_copy(y_v, y_out, side_sem.at[0]), pltpu.make_async_copy(up_v, up_out, side_sem.at[1]),
                    pltpu.make_async_copy(side_v, down_out, side_sem.at[2]))
        for cp in side_in:
            cp.start()
    for cp in idx:
        cp.wait()

    def name_rows(q, carry):
        at = jnp.minimum(pack[head + 16 + q] + rnd * c2, last)
        for j in range(c2):
            col[pl.ds(q * c2 + j, 1), :] = jnp.full((1, LANES), pack[at + j] + q * (vocab * w), I32)
        return carry

    lax.fori_loop(0, n, name_rows, 0)
    many[...] = jnp.zeros(many.shape, F32)
    names = col[:, :1]

    def sum_many(i, carry):
        load(i).wait()
        hot = jnp.where(names == ids[i] * w, 1.0, 0.0).astype(BF16)
        rows = pl.ds(pl.multiple_of(i * step, step), step)
        many[...] += lax.dot_general(hot, dx_v[rows, :], (((1,), (0,)), ((), ())), preferred_element_type=F32)
        split_rows(dx_v.at[rows], dxf, i * step, step)
        return carry

    lax.fori_loop(0, parts, sum_many, 0)
    pltpu.make_async_copy(many, many_out, o_sem.at[1]).start()
    if not again:
        for cp in side_in:
            cp.wait()
        side_v[...] = down_v[...].T
        for cp in side_out:
            cp.start()

    def owner(q, carry):
        at = jnp.minimum(pack[head + q] + rnd * c1, last)
        pick_rows(dxf, g, 0, c1, w, lambda j: toks[at + j])
        join_rows(g, one.at[q], 0, c1)
        pltpu.make_async_copy(one.at[q], one_out.at[q], o_sem.at[0]).start()
        return carry

    lax.fori_loop(0, n, owner, 0)
    pltpu.make_async_copy(one, one_out, o_sem.at[0]).wait()
    pltpu.make_async_copy(many, many_out, o_sem.at[1]).wait()
    if not again:
        for cp in side_out:
            cp.wait()


def collect(n, c1, c2, vocab, rnd, pack, toks, ids, dx, side=None):
    again = side is None
    t, d = dx.shape
    w = d // LANES
    parts = ids.shape[0]
    shapes = (jax.ShapeDtypeStruct((n, c1, d), BF16), jax.ShapeDtypeStruct((n * c2, d), F32))
    extra = []
    if not again:
        y, up, down = side
        shapes += (jax.ShapeDtypeStruct(y.shape, y.dtype), jax.ShapeDtypeStruct(up.shape, F32),
                   jax.ShapeDtypeStruct(down.shape[::-1], F32))
        extra = [pltpu.VMEM(y.shape, y.dtype), pltpu.VMEM(up.shape, F32), pltpu.VMEM(down.shape, F32),
                 pltpu.VMEM(down.shape[::-1], F32), DMA((3,))]
    one, many, *rest = pl.pallas_call(
        functools.partial(collect_kernel, n, c1, c2, vocab, again),
        out_shape=shapes,
        in_specs=[smem_spec(), any_spec(), any_spec(), vmem_spec(), any_spec()] + [any_spec()] * (0 if again else 3),
        out_specs=(any_spec(),) * len(shapes),
        scratch_shapes=[pltpu.SMEM(pack.shape, I32), pltpu.SMEM(toks.shape, I32),
                        pltpu.VMEM((t, d), BF16), pltpu.VMEM((t * w, LANES), F32), pltpu.VMEM((c1 * w, LANES), F32),
                        pltpu.VMEM((n * c2, LANES), I32), pltpu.VMEM((n, c1, d), BF16), pltpu.VMEM((n * c2, d), F32),
                        DMA((2,)), DMA((parts,)), DMA((2,))] + extra,
        compiler_params=pltpu.CompilerParams(vmem_limit_bytes=63 << 20),
        name='collect_more' if again else 'collect_rows',
    )(rnd, pack, toks, ids, dx, *(() if again else side))
    return (one, many.reshape(n, c2, d)) + tuple(rest)


def place_kernel(n, c1, c2, again, *refs):
    if again:
        rnd_ref, who_ref, lists, one_own, many_own, one, many, _, out, ls, acc, o_v, m_v, f_v, st, l_sem, in_sem, out_sem = refs
    else:
        rnd_ref, who_ref, lists, one_own, many_own, one, many, out, ls, acc, o_v, m_v, f_v, st, l_sem, in_sem, out_sem = refs
    me, rnd = who_ref[0], rnd_ref[0]
    vocab, d = out.shape
    w = d // LANES
    asked = pltpu.make_async_copy(lists, ls, l_sem)
    asked.start()
    pl_len = ls.shape[0] // n
    head = pl_len - PAGE

    def load(q):
        return (pltpu.make_async_copy(one.at[q], o_v.at[q], in_sem.at[0, q]),
                pltpu.make_async_copy(many.at[q], m_v.at[q], in_sem.at[1, q]))

    pltpu.make_async_copy(one_own.at[me], o_v.at[me], in_sem.at[0, me]).start()
    pltpu.make_async_copy(many_own.at[me], m_v.at[me], in_sem.at[1, me]).start()
    for k in range(n):
        @pl.when(k != me)
        def _():
            for part in load(k):
                part.start()
    blk = st.shape[1]

    def span(i):
        return pl.ds(pl.multiple_of(i * blk, blk), blk)

    def split8(src, row):
        def one8(r0):
            for k in range(w):
                acc[pl.ds((row + r0) * w + k, 8, stride=w), :] = src[pl.ds(r0, 8), pl.ds(k * LANES, LANES)]
        blocks(blk, 8, 8, one8)

    if again:
        def bring(i, carry):
            pltpu.make_async_copy(out.at[span(i)], st.at[0], out_sem.at[0]).start()
            pltpu.make_async_copy(out.at[span(i)], st.at[0], out_sem.at[0]).wait()
            split8(st.at[0], i * blk)
            return carry

        lax.fori_loop(0, vocab // blk, bring, 0)
    else:
        zero = jnp.zeros((16 * w, LANES), F32)

        def clear(r0):
            acc[pl.ds(r0 * w, 16 * w), :] = zero

        blocks(vocab, 16, 4, clear)
    asked.wait()
    dump = vocab * w

    def add(count, at, row0):
        def body(b, carry):
            lines, sums = [], []
            for u in range(UNROLL):
                j = b * UNROLL + u
                line = pl.multiple_of(jnp.where(j < count, ls[at + j], dump), w)
                lines.append(line)
                src = f_v[pl.ds(pl.multiple_of((row0 + j) * w, w), w), :]
                sums.append(acc[pl.ds(line, w), :] + src)
            for u in range(UNROLL):
                acc[pl.ds(lines[u], w), :] = sums[u]
            return carry

        lax.fori_loop(0, lax.div(count + UNROLL - 1, UNROLL), body, 0)

    def source(q, carry):
        for part in load(q):
            part.wait()
        at = q * pl_len + head
        split_rows(o_v.at[q], f_v, 0, c1)
        split_rows(m_v.at[q], f_v, c1, c2)
        b1, b2 = ls[at + me] + rnd * c1, ls[at + 16 + me] + rnd * c2
        e1, e2 = ls[at + me + 1], ls[at + 16 + me + 1]
        add(jnp.clip(e1 - b1, 0, c1), q * pl_len + b1, 0)
        add(jnp.clip(e2 - b2, 0, c2), q * pl_len + b2, c1)
        return carry

    lax.fori_loop(0, n, source, 0)

    def emit(i, carry):
        slot = lax.rem(i, 2)

        @pl.when(i >= 2)
        def _():
            pltpu.make_async_copy(st.at[slot], out.at[span(i - 2)], out_sem.at[slot]).wait()

        def one8(r0):
            for k in range(w):
                st[slot, pl.ds(r0, 8), pl.ds(k * LANES, LANES)] = acc[pl.ds((i * blk + r0) * w + k, 8, stride=w), :]

        blocks(blk, 8, 8, one8)
        pltpu.make_async_copy(st.at[slot], out.at[span(i)], out_sem.at[slot]).start()
        return carry

    total = vocab // blk
    lax.fori_loop(0, total, emit, 0)
    for i in range(max(0, total - 2), total):
        pltpu.make_async_copy(st.at[i % 2], out.at[span(i)], out_sem.at[i % 2]).wait()


def place(n, c1, c2, vocab, rnd, who, lists, one_own, many_own, one, many, prev=None):
    again = prev is not None
    d = one.shape[-1]
    w = d // LANES
    blk = next(b for b in range(1280, 0, -8) if vocab % b == 0)
    return pl.pallas_call(
        functools.partial(place_kernel, n, c1, c2, again),
        out_shape=jax.ShapeDtypeStruct((vocab, d), F32),
        in_specs=[smem_spec()] * 2 + [any_spec()] * (6 if again else 5),
        out_specs=any_spec(),
        scratch_shapes=[
            pltpu.SMEM(lists.shape, I32), pltpu.VMEM((vocab * w + 8, LANES), F32), pltpu.VMEM((n, c1, d), BF16), pltpu.VMEM((n, c2, d), F32),
            pltpu.VMEM(((c1 + c2) * w, LANES), F32), pltpu.VMEM((2, blk, d), F32), DMA, DMA((2, n)), DMA((2,)),
        ],
        input_output_aliases={7: 0} if again else {},
        compiler_params=pltpu.CompilerParams(vmem_limit_bytes=63 << 20),
        name='place_more' if again else 'place_rows',
    )(rnd, who, lists, one_own, many_own, one, many, *((prev,) if again else ()))


def route(n, vocab, w, c1, c2, ids):
    t = ids.shape[0]
    c = c1 + c2
    s, p = lax.sort((ids, lax.iota(I32, t)), num_keys=1)
    edge = jnp.full((1,), -1, I32)
    first = s != jnp.concatenate([edge, s[:-1]])
    last = s != jnp.concatenate([s[1:], edge])
    lone = first & last
    lead = first & ~last
    lone_i, lead_i = lone.astype(I32), lead.astype(I32)
    bounds = lax.iota(I32, n + 1) * vocab
    below = s[None, :] < bounds[:, None]
    base1 = jnp.sum(jnp.where(below, lone_i[None, :], 0), axis=1)
    base2 = jnp.sum(jnp.where(below, lead_i[None, :], 0), axis=1)
    owner = n - jnp.sum(below[1:].astype(I32), axis=0)
    mine = owner[None, :] == lax.iota(I32, n)[:, None]
    start1 = jnp.sum(jnp.where(mine, base1[:n, None], 0), axis=0)
    start2 = jnp.sum(jnp.where(mine, base2[:n, None], 0), axis=0)
    r1 = jnp.cumsum(lone_i) - lone_i - start1
    r2 = jnp.cumsum(lead_i) - 1 - start2
    rnd1, rnd2 = r1 // c1, r2 // c2
    slot = jnp.where(lone, rnd1 * (n * c) + owner * c + r1 - rnd1 * c1, rnd2 * (n * c) + owner * c + c1 + r2 - rnd2 * c2)
    kind = jnp.where(lone, 0, jnp.where(lead, 1, 2)) * t + lax.iota(I32, t)
    _, line, tok = lax.sort((kind, (s - owner * vocab) * w, p * w), num_keys=1)
    n1 = base1[n]
    room = -(-(t + c1 + c2) // PAGE) * PAGE
    spare = jnp.zeros((16 - n - 1,), I32)
    heads = jnp.concatenate([base1, spare, n1 + base2, spare])
    fill = jnp.zeros((room - t,), I32)
    heads = jnp.concatenate([heads, jnp.zeros((PAGE - heads.shape[0],), I32)])
    pack = jnp.concatenate([line, fill, heads])
    lone_tok = jnp.concatenate([tok, fill])
    per1 = jnp.max(base1[1:] - base1[:-1])
    per2 = jnp.max(base2[1:] - base2[:-1])
    rounds = jnp.maximum((per1 + c1 - 1) // c1, (per2 + c2 - 1) // c2)
    return pack, lone_tok, p * w, slot * w, rounds


def solution(mesh):
    n = mesh.shape[AXIS]
    axes = tuple(mesh.axis_names)
    others = tuple((name, mesh.shape[name]) for name in axes if name != AXIS)
    tok_spec = P(axes)
    row_spec = P(axes, None)

    def local_step(token_ids, emb_shard, norm_gain, w_up_l, w_down_l, grad_out):
        vocab, d = emb_shard.shape
        t = token_ids.shape[0]
        w = d // LANES
        c1 = -(-(t * 5 // (8 * n)) // 16) * 16
        c2 = -(-(t // 128) // 16) * 16
        who = lax.axis_index(AXIS)[None].astype(I32)
        w_up = lax.all_gather(w_up_l, AXIS)
        w_down = lax.all_gather(w_down_l, AXIS)
        pack, lone_tok, toks, lines, rounds = route(n, vocab, w, c1, c2, token_ids)
        lists = share(n, pack)
        none = jnp.zeros((1,), I32)

        def rows_of(rnd):
            sent = serve(n, c1, c2, rnd, who, lists, emb_shard)
            return sent, swap(n, 2, 'swap_rows', sent)[0]

        def more_rows(carry):
            r, x_now = carry
            return r + 1, expand(n, r[None], who, toks, lines, *rows_of(r[None]), x_now)

        sent = serve(n, c1, c2, none, who, lists, emb_shard)
        got, most, dh, dot = swap_first(n, others, sent, jnp.full((8, LANES), rounds, I32), grad_out, w_down)
        rounds = most[0, 0]
        x = expand(n, none, who, toks, lines, sent, got)
        _, x = lax.while_loop(lambda carry: carry[0] < rounds, more_rows, (jnp.ones((), I32), x))
        out, dx, dw1, dw2t = mlp(n, 4, x, norm_gain, w_up, w_down, grad_out, dh, dot)
        ids_c = token_ids.reshape(-1, 1, t // 8)

        one, many, out, dw1, dw2 = collect(n, c1, c2, vocab, none, pack, lone_tok, ids_c, dx, (out, dw1, dw2t))

        def more_sums(carry):
            r, now = carry
            mine = collect(n, c1, c2, vocab, r[None], pack, lone_tok, ids_c, dx)
            return r + 1, place(n, c1, c2, vocab, r[None], who, lists, *mine, *swap(n, 3, 'swap_sums', *mine), now)

        d_emb = place(n, c1, c2, vocab, none, who, lists, one, many, *swap(n, 3, 'swap_sums', one, many))
        _, d_emb = lax.while_loop(lambda carry: carry[0] < rounds, more_sums, (jnp.ones((), I32), d_emb))
        return out, d_emb, dw1, dw2

    return jax.shard_map(
        local_step,
        mesh=mesh,
        in_specs=(tok_spec, P(AXIS, None), P(None), P(None, AXIS), P(AXIS, None), row_spec),
        out_specs=(row_spec, row_spec, P(axes[0], AXIS), row_spec),
        check_vma=False,
    )
```

time: 343 us -> 250 us (0.73)
  Pallas kernels: 284 us -> 211 us
  local copies, waits for them, and re-layouts: 16.8 us -> 4.09 us
  other arithmetic: 22.6 us -> 15.9 us
    pallas_call x2 -> x1, Pallas kernels: 90.3 us -> 40 us  [swap(): pl.pallas_call(functools.partial(swap_kernel, n, m), out_shape=tuple((jax...]
    pallas_call x1, Pallas kernels: 55.8 us -> 15.5 us  [place(): pl.pallas_call(functools.partial(place_kernel, n, c1, c2, again), out_sha...]
    pallas_call x2 -> x3, Pallas kernels: 23.4 us -> 58.6 us  [the longest x1 39.5 us: swap_first(): pl.pallas_call(functools.partial(swap_first_kernel, n, others, tc), out_s...]
    unnamed x21 -> x2, local copies, waits for them, and re-layouts: 11.2 us -> 0.01 us
    pallas_call x1, Pallas kernels: 18.6 us -> 10.6 us  [expand(): pl.pallas_call(functools.partial(expand_kernel, n, c, again), out_shape=j...]
    concatenate x1 -> x0, other arithmetic: 7.23 us -> none  [local_step(): jnp.concatenate([dw1, dw2t], axis=1)]
    pallas_call x1, Pallas kernels: 84.4 us -> 77.5 us  [mlp(): pl.pallas_call(functools.partial(mlp_kernel, n, tc), out_shape=(jax.Shape...]
  transfers between devices with their start and end apart: 3 -> 2, of which waited for: 0 -> 0; matrix products, arithmetic and copies ran while one was open for 6% -> 8% of each run, Pallas kernels for 58% -> 27%
where the time goes in v2:
time: 250 us
  Pallas kernels  211 us (84%)
  other arithmetic  15.9 us (6%)
  between operations  15.6 us (6%)
  local copies, waits for them, and re-layouts  4.09 us (2%)
    pallas_call x1, Pallas kernels, mlp(): pl.pallas_call(functools.partial(mlp_kernel, n, tc), out_shape=(jax.Shape...  77.5 us
    pallas_call x1, Pallas kernels, swap(): pl.pallas_call(functools.partial(swap_kernel, n, m), out_shape=tuple((jax...  40 us
    pallas_call x1, Pallas kernels, swap_first(): pl.pallas_call(functools.partial(swap_first_kernel, n, others, tc), out_s...  39.5 us
    pallas_call x1, Pallas kernels, place(): pl.pallas_call(functools.partial(place_kernel, n, c1, c2, again), out_sha...  15.5 us
    pallas_call x1, Pallas kernels, expand(): pl.pallas_call(functools.partial(expand_kernel, n, c, again), out_shape=j...  10.6 us
    pallas_call x1, Pallas kernels, collect(): pl.pallas_call(functools.partial(collect_kernel, n, c1, c2, vocab, again)...  10.4 us
    pallas_call x1, Pallas kernels, serve(): pl.pallas_call(functools.partial(serve_kernel, n, c1, c2), out_shape=jax....  9.08 us
    pallas_call x1, Pallas kernels, share(): pl.pallas_call(functools.partial(share_kernel, n), out_shape=jax.ShapeDty...  8.75 us
  transfers between devices with their start and end apart: 2, of which 0 were waited for; matrix products, arithmetic and copies ran while one was open for 8% of the time, Pallas kernels for 27%

profile of v2, /device:TPU:113, one launch (start us, length us, event | category | flops | bytes accessed | tf_op | source)
XLA Modules:
  0.0 249.8 jit_solution(2221260561585982958)
XLA Ops:
  7.2 0.1 all-gather.5.cloned.1.call-start
  7.2 0.7 all-gather.5.cloned.1.call-update
  8.0 0.1 all-gather.7.cloned.1.call-start
  8.0 0.7 all-gather.7.cloned.1.call-update
  8.8 5.9 %sort.46 = (s32[4096]{0:T(1024)S(1)}, s32[4096]{0:T(1024)S(1)}) sort(s32[4096]{0:T(1024)} %param.10, s32[4096]{0:T(1024)S(1)} %iota.18), dimensions={0}, to_apply=%region_0.0 | sort | flops 49152 | bytes 65536 | tf_op jit(solution)/shard_map/sort | solution.py:858
  14.7 0.1 fusion.8
  14.8 0.1 convert_bitcast_fusion.1
  14.9 0.3 select_reduce_fusion
  15.1 0.7 subtract_reduce_fusion
  17.2 0.6 slice.46
  17.8 0.3 reduce-window.16
  18.1 0.1 slice.57
  18.2 0.1 reduce-window.19
  18.2 0.3 reduce-window.24
  18.5 0.1 slice.59
  18.6 0.1 reduce-window.25
  18.6 0.1 slice_reduce_fusion
  18.8 0.1 broadcast_compare_fusion
  18.9 0.1 convert_reduce_fusion
  18.9 0.1 select_reduce_fusion.2
  19.1 0.7 fusion.5
  19.8 0.6 fusion.6
  20.4 5.9 %sort.47 = (s32[4096]{0:T(1024)}, s32[4096]{0:T(1024)S(1)}, s32[4096]{0:T(1024)S(1)}, s32[4096]{0:T(1024)}) sort(s32[4096]{0:T(1024)S(1)} %get-tuple-element.195, s32[4096]{0:T(1024)S(1)} %get-tuple-element.191, s32[4096]{0:T(1024)S(1)} %get-tuple-element.326, s32[4096]{0:T(1024)S(1)} %iota.21), dimensions={0}, to_apply=%region_2.3 | sort | flops 49152 | bytes 131072 | tf_op jit(solution)/shard_map/sort | solution.py:878
  26.4 0.7 broadcast_add_fusion
  27.1 0.1 concatenate.14.pack.refs_1_
  27.2 8.8 %share_lists.1.lists.refs_2_ = s32[49152]{0:T(1024)S(1)} custom-call(s32[6144]{0:T(1024)S(1)} %concatenate.14.pack.refs_1_), custom_call_target="tpu_custom_call" | custom-call | tf_op jit(solution)/shard_map/share_lists/pallas_call | solution.py:349
  35.9 1.2 reshape.67.g_ref
  37.2 9.1 %serve_rows.2.sent.refs_3_ = bf16[8,352,512]{2,1,0:T(8,128)(2,1)} custom-call(s32[1]{0:T(128)} %constant.41.clone.1.rnd_ref.refs_0_, s32[1]{0:T(128)} %bitcast.5.who_ref.refs_0_.refs_1_, s32[49152]{0:T(1024)S(1)} %share_lists.1.lists.refs_2_, bf16[6288,512]{1,0:T(8,128)(2,1)} %table.1), custom_call_target="tpu_custom_call" | custom-call | tf_op jit(solution)/shard_map/serve_rows/pallas_call | solution.py:401
  46.2 0.0 all-gather.5.cloned.1.call-done
  46.3 0.6 broadcast_in_dim.98.need
  46.9 39.5 %swap_first.1 = (bf16[8,352,512]{2,1,0:T(8,128)(2,1)}, s32[8,128]{1,0:T(8,128)}, f32[8,4096,256]{2,1,0:T(8,128)}, bf16[512,4096]{1,0:T(8,128)(2,1)}) custom-call(bf16[8,352,512]{2,1,0:T(8,128)(2,1)} %serve_rows.2.sent.refs_3_, s32[8,128]{1,0:T(8,128)} %broadcast_in_dim.98.need, bf16[4096,512]{1,0:T(8,128)(2,1)} %do_hbm.3, bf16[8,256,512]{2,1,0:T(8,128)(2,1)} %bitcast.36), custom_call_target="tpu_custom_call" | custom-call | tf_op jit(solution)/shard_map/swap_first/pallas_call | solution.py:538
  86.4 1.2 slice.55
  87.5 10.6 %expand_rows.1 = bf16[4096,512]{1,0:T(8,128)(2,1)} custom-call(s32[1]{0:T(128)} %bitcast.5.who_ref.refs_0_.refs_1_, s32[4096]{0:T(1024)} %get-tuple-element.189.refs_1_, s32[4096]{0:T(1024)} %get-tuple-element.180.refs_2_, bf16[8,352,512]{2,1,0:T(8,128)(2,1)} %serve_rows.2.sent.refs_3_, bf16[8,352,512]{2,1,0:T(8,128)(2,1)} %get-tuple-element.125.refs_4_), custom_call_target="tpu_custom_call" | custom-call | tf_op jit(solution)/shard_map/expand_rows/pallas_call | solution.py:615
  98.2 0.7 while.20
  98.9 0.0 all-gather.7.cloned.1.call-done
  99.0 0.0 copy-start
  99.0 77.5 %mlp_block.1 = (bf16[4096,512]{1,0:T(8,128)(2,1)}, bf16[4096,512]{1,0:T(8,128)(2,1)}, f32[512,256]{1,0:T(8,128)}, f32[512,256]{1,0:T(8,128)}) custom-call(bf16[4096,512]{1,0:T(8,128)(2,1)} %get-tuple-element.127.x_hbm, bf16[1,512]{1,0:T(2,128)(2,1)} %reshape.67.g_ref, bf16[8,512,256]{2,1,0:T(8,128)(2,1)} %bitcast.40, bf16[8,256,512]{2,1,0:T(8,128)(2,1)} %bitcast.37, ...), custom_call_target="tpu_custom_call" | custom-call | flops 51539607552 | bytes 41943040 | tf_op jit(solution)/shard_map/mlp_block/pallas_call | solution.py:301
  176.4 0.0 copy-done
  176.5 10.4 %collect_rows.1 = (bf16[8,320,512]{2,1,0:T(8,128)(2,1)}, f32[256,512]{1,0:T(8,128)}, bf16[4096,512]{1,0:T(8,128)(2,1)}, f32[512,256]{1,0:T(8,128)}, f32[256,512]{1,0:T(8,128)}) custom-call(s32[1]{0:T(128)} %constant.41.clone.1.rnd_ref.refs_0_, s32[6144]{0:T(1024)S(1)} %concatenate.14.pack.refs_1_, s32[5120]{0:T(1024)S(1)} %concatenate.15.refs_2_, ...), custom_call_target="tpu_custom_call" | custom-call | tf_op jit(solution)/shard_map/collect_rows/pallas_call | solution.py:717
  186.9 40.0 %swap_sums.2 = (bf16[8,320,512]{2,1,0:T(8,128)(2,1)}, f32[8,32,512]{2,1,0:T(8,128)}) custom-call(bf16[8,320,512]{2,1,0:T(8,128)(2,1)} %get-tuple-element.135.refs_0_.refs_3_, f32[8,32,512]{2,1,0:T(8,128)} %bitcast.34), custom_call_target="tpu_custom_call" | custom-call | tf_op jit(solution)/shard_map/swap_sums/pallas_call | solution.py:433
  226.8 15.5 %place_rows.1 = f32[6288,512]{1,0:T(8,128)} custom-call(s32[1]{0:T(128)} %constant.41.clone.1.rnd_ref.refs_0_, s32[1]{0:T(128)} %bitcast.5.who_ref.refs_0_.refs_1_, s32[49152]{0:T(1024)S(1)} %get-tuple-element.384, bf16[8,320,512]{2,1,0:T(8,128)(2,1)} %get-tuple-element.135.refs_0_.refs_3_, f32[8,32,512]{2,1,0:T(8,128)} %bitcast.35, ...), custom_call_target="tpu_custom_call" | custom-call | tf_op jit(solution)/shard_map/place_rows/pallas_call | solution.py:840
  242.4 0.6 while.21
  (10 shorter events, 0.0 us)
Async XLA Ops:
  7.2 39.1 %all-gather.5.cloned.1.call-start = ((), (), s32[]{:S(2)}) async-start(), calls=%async_computation | async-start | bytes 2359296 | tf_op jit(solution)/shard_map/all_gather | solution.py:908
  8.0 91.0 %all-gather.7.cloned.1.call-start = ((), (), s32[]{:S(2)}) async-start(), calls=%async_computation.1 | async-start | bytes 2359296 | tf_op jit(solution)/shard_map/all_gather | solution.py:907
  99.0 77.5 %copy-start = (s32[4096]{0:T(1024)S(1)}, s32[4096]{0:T(1024)}, u32[]{:S(2)}) copy-start(s32[4096]{0:T(1024)} %param.10) | copy-start | bytes 49156
Sparse Core Ops, SparseCore 0:
  9.6 24.5 all-gather.4
  35.8 34.0 all-gather.6

commit v3 on v2

--- a/solution.py
+++ b/solution.py
@@ -13,7 +13,8 @@
 I32 = jnp.int32
 MESH = pl.DeviceIdType.MESH
 LANES = 128
-UNROLL = 16
+UNROLL = 32
+UNROLL_ADD = 8
 PAGE = 1024
 AXIS = 'tensor'
 
@@ -113,14 +114,15 @@
     return h.astype(BF16), (dh * slope).astype(BF16)
 
 
-def mlp_kernel(n, tc, x_hbm, g_ref, w1_hbm, w2_hbm, do_hbm, dh_hbm, dot_hbm, out_hbm, dx_hbm, dw1_hbm, dw2_hbm,
-               x_v, do_v, n_v, nt_v, dot_v, y_v, dn_v, w1_ref, w2_ref, h_a, h_b, du_a, du_b, dh_a, dh_b, part, mate, ours, theirs,
+def mlp_kernel(n, tc, x_hbm, g_ref, w_hbm, do_hbm, dh_hbm, dot_hbm, out_hbm, dx_hbm, dw1_hbm, dw2_hbm,
+               x_v, do_v, n_v, nt_v, dot_v, y_v, dn_v, w_ref, h_a, h_b, du_a, du_b, dh_a, dh_b, part, mate, ours, theirs,
                in_sem, w_sem, dh_sem, out_sem, dw_sem, ms, mr, cs, cr):
     me = lax.axis_index(AXIS)
     core, chip = lax.rem(me, 2), lax.div(me, 2)
     chips = n // 2
     far = sorted(range(1, chips), key=lambda k: -min(k, chips - k)) + [0]
     t_all, d = x_v.shape
+    fs = w_ref.shape[2] // 2
     nc = t_all // tc
     rows = lambda c: pl.ds(pl.multiple_of(c * tc, tc), tc)
     mate_id = {AXIS: me + 1 - 2 * core}
@@ -131,21 +133,23 @@
 
     for c in range(nc):
         load(c).start()
-    weights = (pltpu.make_async_copy(w1_hbm, w1_ref, w_sem.at[0]), pltpu.make_async_copy(w2_hbm, w2_ref, w_sem.at[1]),
-               pltpu.make_async_copy(dot_hbm, dot_v, w_sem.at[2]))
+    weights = (pltpu.make_async_copy(w_hbm, w_ref, w_sem.at[0]), pltpu.make_async_copy(dot_hbm, dot_v, w_sem.at[2]))
     for cp in weights:
         cp.start()
     group_barrier(n, me, wait=False)
     late = pltpu.make_async_copy(do_hbm, do_v, w_sem.at[3])
     late.start()
 
+    def offset(q, which):
+        off = sum(jnp.where(q == i, k, 0) for i, k in enumerate(far))
+        return jnp.where(which == 0, off, lax.rem(chips - off, chips))
+
     def owner_chip(q):
-        off = sum(jnp.where(q == i, k, 0) for i, k in enumerate(far))
-        return lax.rem(chip + off, chips)
+        return lax.rem(chip + offset(q, core), chips)
 
     def block_of(jj):
         half = lax.rem(jj, 2)
-        return 2 * owner_chip(lax.div(jj, 2)) + jnp.where(half == 0, 1 - core, core)
+        return 1 - half, offset(lax.div(jj, 2), jnp.where(half == 0, 1 - core, core))
 
     def mate_copy(q):
         return pltpu.make_async_remote_copy(part.at[0], mate.at[q], ms.at[q], mr.at[q],
@@ -172,8 +176,8 @@
     hs, dus, dhs = (h_a, h_b), (du_a, du_b), (dh_a, dh_b)
 
     def pull(i, slot):
-        j, c = block_of(lax.div(i, nc)), lax.rem(i, nc)
-        return pltpu.make_async_copy(dh_hbm.at[j, rows(c)], dhs[slot], dh_sem.at[slot])
+        (side, rel), c = block_of(lax.div(i, nc)), lax.rem(i, nc)
+        return pltpu.make_async_copy(dh_hbm.at[side * chips + rel, rows(c)], dhs[slot], dh_sem.at[slot])
 
     for i in range(2):
         pull(i, i).start()
@@ -186,19 +190,20 @@
     sub = tc // 4
 
     def first_piece(i, slot, k):
-        j, c = block_of(lax.div(i, nc)), lax.rem(i, nc)
+        (side, rel), c = block_of(lax.div(i, nc)), lax.rem(i, nc)
         here = pl.ds(k * sub, sub)
-        u = dot_nn(n_v[pl.ds(pl.multiple_of(c * tc + k * sub, sub), sub), :], w1_ref[j]).astype(BF16).astype(F32)
+        u = dot_nt(n_v[pl.ds(pl.multiple_of(c * tc + k * sub, sub), sub), :], w_ref[side, rel, pl.ds(0, fs), :])
+        u = u.astype(BF16).astype(F32)
         hs[slot][here, :], dus[slot][here, :] = gelu_pair(u, dhs[slot][here, :])
 
     def second_piece(i, slot, k):
         jj, c = lax.div(i, nc), lax.rem(i, nc)
-        j, half = block_of(jj), lax.rem(jj, 2)
+        (side, rel), half = block_of(jj), lax.rem(jj, 2)
         r = rows(c)
         if k == 0:
-            y_v[r, :] += dot_nn(hs[slot][...], w2_ref[j])
+            y_v[r, :] += dot_nn(hs[slot][...], w_ref[side, rel, pl.ds(fs, fs), :])
         elif k == 1:
-            dn_v[r, :] += dot_nt(dus[slot][...], w1_ref[j])
+            dn_v[r, :] += dot_nn(dus[slot][...], w_ref[side, rel, pl.ds(0, fs), :])
         elif k == 2:
             part[half, 0] += dot_nn(nt_v[:, r], dus[slot][...])
         else:
@@ -293,9 +298,9 @@
     pltpu.make_async_copy(x_v, out_hbm, out_sem.at[0]).wait()
 
 
-def mlp(n, cid, x, g, w1s, w2s, dout, dh, dot, tc=1024):
+def mlp(n, cid, x, g, ws, dout, dh, dot, tc=1024):
     t, d = x.shape
-    fs = w1s.shape[2]
+    fs = dh.shape[2]
     nc = t // tc
     chips = n // 2
     return pl.pallas_call(
@@ -306,13 +311,13 @@
             jax.ShapeDtypeStruct((d, fs), F32),
             jax.ShapeDtypeStruct((d, fs), F32),
         ),
-        in_specs=[any_spec(), vmem_spec()] + [any_spec()] * 5,
+        in_specs=[any_spec(), vmem_spec()] + [any_spec()] * 4,
         out_specs=(any_spec(),) * 4,
         scratch_shapes=[
             pltpu.VMEM((t, d), BF16), pltpu.VMEM((t, d), BF16), pltpu.VMEM((t, d), BF16),
             pltpu.VMEM((d, t), BF16), pltpu.VMEM((d, t), BF16),
             pltpu.VMEM((t, d), F32), pltpu.VMEM((t, d), F32),
-            pltpu.VMEM(w1s.shape, BF16), pltpu.VMEM(w2s.shape, BF16),
+            pltpu.VMEM(ws.shape, BF16),
             pltpu.VMEM((tc, fs), BF16), pltpu.VMEM((tc, fs), BF16), pltpu.VMEM((tc, fs), BF16), pltpu.VMEM((tc, fs), BF16),
             pltpu.VMEM((tc, fs), F32), pltpu.VMEM((tc, fs), F32),
             pltpu.VMEM((2, 2, d, fs), F32), pltpu.VMEM((chips, 2, d, fs), F32),
@@ -323,10 +328,10 @@
             collective_id=cid, has_side_effects=True, vmem_limit_bytes=63 << 20),
         cost_estimate=pl.CostEstimate(flops=12 * t * d * n * fs, bytes_accessed=40 << 20, transcendentals=t * n * fs),
         name='mlp_block',
-    )(x, g.reshape(1, d), w1s, w2s, dout, dh, dot)
-
-
-def share_kernel(n, pack, lists, ss, rs, own_sem):
+    )(x, g.reshape(1, d), ws, dout, dh, dot)
+
+
+def share_kernel(n, fs, pack, behind, before, lists, across, ss, rs, own_sem, fs_sem, fr_sem):
     me = lax.axis_index(AXIS)
     pl_len = pack.shape[0]
     here = pl.ds(pl.multiple_of(me * pl_len, PAGE), pl_len)
@@ -338,23 +343,32 @@
         return pltpu.make_async_remote_copy(pack, lists.at[here], ss.at[k], rs.at[k],
                                             device_id={AXIS: lax.rem(me + k, n)}, device_id_type=MESH)
 
+    def forward(way, src):
+        half = pl.ds(way * fs, fs)
+        return pltpu.make_async_remote_copy(src.at[half], across.at[half], fs_sem.at[way], fr_sem.at[way],
+                                            device_id={AXIS: lax.rem(me + (2 if way == 0 else n - 2), n)}, device_id_type=MESH)
+
     for k in far_first(n):
         list_copy(k).start()
+    forward(0, behind).start()
+    forward(1, before).start()
     for k in far_first(n):
         list_copy(k).wait()
     own.wait()
-
-
-def share(n, pack):
+    forward(0, behind).wait()
+    forward(1, before).wait()
+
+
+def share(n, pack, behind, before):
     return pl.pallas_call(
-        functools.partial(share_kernel, n),
-        out_shape=jax.ShapeDtypeStruct((n * pack.shape[0],), I32),
-        in_specs=[any_spec()],
-        out_specs=any_spec(),
-        scratch_shapes=[DMA((n,)), DMA((n,)), DMA],
+        functools.partial(share_kernel, n, behind.shape[0] // 2),
+        out_shape=(jax.ShapeDtypeStruct((n * pack.shape[0],), I32), jax.ShapeDtypeStruct(behind.shape, BF16)),
+        in_specs=[any_spec()] * 3,
+        out_specs=(any_spec(),) * 2,
+        scratch_shapes=[DMA((n,)), DMA((n,)), DMA, DMA((2,)), DMA((2,))],
         compiler_params=pltpu.CompilerParams(collective_id=1, has_side_effects=True, vmem_limit_bytes=63 << 20),
         name='share_lists',
-    )(pack)
+    )(pack, behind, before)
 
 
 def serve_kernel(n, c1, c2, rnd_ref, who_ref, lists, table, out, ls, e_st, ef, g, sent, l_sem, e_sem, o_sem):
@@ -441,10 +455,13 @@
     )(*arrays)
 
 
-def swap_first_kernel(n, others, tc, sent, need, do_hbm, w2_hbm, got, most, dh_hbm, dot_hbm, do_v, w2_v, dot_v, dh_v,
-                      peers, relay, ss, rs, ns, nr, xs_sem, xr_sem, in_sem, w_sem, dh_sem, dot_sem):
+def swap_first_kernel(n, others, tc, spots, sent, need, do_hbm, *refs):
+    pieces, refs = refs[:len(spots)], refs[len(spots):]
+    (got, most, dh_hbm, dot_hbm, w_hbm, do_v, w_v, dot_v, dh_v, peers, relay,
+     ss, rs, ns, nr, xs_sem, xr_sem, in_sem, w_sem, dh_sem, dot_sem, ms, mr, wo_sem) = refs
     me = lax.axis_index(AXIS)
     t, d = do_v.shape
+    chips, fs = w_v.shape[1], w_v.shape[2] // 2
     nc = t // tc
     rows = lambda c: pl.ds(pl.multiple_of(c * tc, tc), tc)
     hops = []
@@ -454,11 +471,20 @@
             hops.append((name, size, reach))
             reach *= 2
 
+    def piece(i):
+        rel, row = spots[i]
+        size = pieces[i].shape[0]
+        return pltpu.make_async_copy(pieces[i], w_v.at[0, rel, pl.ds(row, size)], w_sem.at[i])
+
+    def mate_copy(rel):
+        return pltpu.make_async_remote_copy(w_v.at[0, rel], w_v.at[1, rel], ms.at[rel], mr.at[rel],
+                                            device_id={AXIS: me + 1 - 2 * lax.rem(me, 2)}, device_id_type=MESH)
+
     def load(c):
         return pltpu.make_async_copy(do_hbm.at[rows(c)], do_v.at[rows(c)], in_sem.at[c])
 
-    weights = pltpu.make_async_copy(w2_hbm, w2_v, w_sem)
-    weights.start()
+    for i in range(len(spots)):
+        piece(i).start()
     for c in range(nc):
         load(c).start()
     sem = pltpu.get_barrier_semaphore()
@@ -482,16 +508,28 @@
         need_copy(k).start()
     for k in far_first(n):
         row_copy(k).start()
-    weights.wait()
+    for i in range(len(spots)):
+        piece(i).wait()
+    for rel in range(chips):
+        mate_copy(rel).start()
+    kept = pltpu.make_async_copy(w_v.at[0], w_hbm.at[0], wo_sem.at[0])
+    kept.start()
+    taken = pltpu.make_async_copy(w_v.at[1], w_hbm.at[1], wo_sem.at[1])
 
     def put(i):
-        return pltpu.make_async_copy(dh_v.at[lax.rem(i, 2)], dh_hbm.at[lax.rem(i, n), rows(lax.div(i, n))],
+        return pltpu.make_async_copy(dh_v.at[lax.rem(i, 2)], dh_hbm.at[lax.div(i, nc), rows(lax.rem(i, nc))],
                                      dh_sem.at[lax.rem(i, 2)])
 
     def body(i, carry):
-        c, j = lax.div(i, n), lax.rem(i, n)
-
-        @pl.when(j == 0)
+        s, c = lax.div(i, nc), lax.rem(i, nc)
+
+        @pl.when(i == nc * chips)
+        def _():
+            for rel in range(chips):
+                mate_copy(rel).wait_recv()
+            taken.start()
+
+        @pl.when(s == 0)
         def _():
             load(c).wait()
             dot_v[:, rows(c)] = do_v[rows(c), :].T
@@ -500,7 +538,7 @@
         def _():
             put(i - 2).wait()
 
-        dh_v[lax.rem(i, 2)] = dot_nt(do_v[rows(c), :], w2_v[j])
+        dh_v[lax.rem(i, 2)] = dot_nt(do_v[rows(c), :], w_v[lax.div(s, chips), lax.rem(s, chips), pl.ds(fs, fs), :])
         put(i).start()
         return carry
 
@@ -524,31 +562,55 @@
     for i in range(steps - 2, steps):
         put(i).wait()
     turned.wait()
+    kept.wait()
+    taken.wait()
+    for rel in range(chips):
+        mate_copy(rel).wait_send()
     for k in far_first(n):
         need_copy(k).wait_send()
         row_copy(k).wait()
 
 
-def swap_first(n, others, sent, need, dout, w2s, tc=1024):
+def swap_first(n, others, sent, need, dout, pieces, spots, tc=1024):
     t, d = dout.shape
-    fs = w2s.shape[1]
+    fs = pieces[0].shape[0] // 2
+    chips = n // 2
     nc = t // tc
     hops = max(1, sum((size - 1).bit_length() for _, size in others))
     tile = (8, LANES)
+    w_shape = (2, chips, 2 * fs, d)
     return pl.pallas_call(
-        functools.partial(swap_first_kernel, n, others, tc),
+        functools.partial(swap_first_kernel, n, others, tc, spots),
         out_shape=(jax.ShapeDtypeStruct(sent.shape, sent.dtype), jax.ShapeDtypeStruct(tile, I32),
-                   jax.ShapeDtypeStruct((n, t, fs), F32), jax.ShapeDtypeStruct((d, t), BF16)),
-        in_specs=[any_spec(), vmem_spec(), any_spec(), any_spec()],
-        out_specs=(any_spec(), vmem_spec(), any_spec(), any_spec()),
+                   jax.ShapeDtypeStruct((n, t, fs), F32), jax.ShapeDtypeStruct((d, t), BF16),
+                   jax.ShapeDtypeStruct(w_shape, BF16)),
+        in_specs=[any_spec(), vmem_spec(), any_spec()] + [any_spec()] * len(pieces),
+        out_specs=(any_spec(), vmem_spec(), any_spec(), any_spec(), any_spec()),
         scratch_shapes=[
-            pltpu.VMEM((t, d), BF16), pltpu.VMEM(w2s.shape, BF16), pltpu.VMEM((d, t), BF16), pltpu.VMEM((2, tc, fs), F32),
+            pltpu.VMEM((t, d), BF16), pltpu.VMEM(w_shape, BF16), pltpu.VMEM((d, t), BF16), pltpu.VMEM((2, tc, fs), F32),
             pltpu.VMEM((n,) + tile, I32), pltpu.VMEM((2 * hops,) + tile, I32),
-            DMA((n,)), DMA((n,)), DMA((n,)), DMA((n,)), DMA((hops,)), DMA((hops,)), DMA((nc,)), DMA, DMA((2,)), DMA,
+            DMA((n,)), DMA((n,)), DMA((n,)), DMA((n,)), DMA((hops,)), DMA((hops,)), DMA((nc,)), DMA((len(pieces),)),
+            DMA((2,)), DMA, DMA((chips,)), DMA((chips,)), DMA((2,)),
         ],
         compiler_params=pltpu.CompilerParams(collective_id=5, has_side_effects=True, vmem_limit_bytes=63 << 20),
         name='swap_first',
-    )(sent, need, dout, w2s)
+    )(sent, need, dout, *pieces)
+
+
+def gather_weights(n, w_up_l, w_down_l):
+    chips = n // 2
+    fs = w_down_l.shape[0]
+    ahead = [(i, (i + 2) % n) for i in range(n)]
+    back = [(i, (i - 2) % n) for i in range(n)]
+    own = jnp.concatenate([w_up_l.T, w_down_l], axis=0)
+    pieces, spots = [own], [(0, 0)]
+    behind = before = own
+    for k in range(1, (chips - 1) // 2 + 1):
+        behind = lax.ppermute(behind, AXIS, ahead)
+        before = lax.ppermute(before, AXIS, back)
+        pieces += [behind, before]
+        spots += [(chips - k, 0), (k, 0)]
+    return tuple(pieces), tuple(spots)
 
 
 def expand_kernel(n, c, again, *refs):
@@ -785,17 +847,17 @@
     def add(count, at, row0):
         def body(b, carry):
             lines, sums = [], []
-            for u in range(UNROLL):
-                j = b * UNROLL + u
+            for u in range(UNROLL_ADD):
+                j = b * UNROLL_ADD + u
                 line = pl.multiple_of(jnp.where(j < count, ls[at + j], dump), w)
                 lines.append(line)
                 src = f_v[pl.ds(pl.multiple_of((row0 + j) * w, w), w), :]
                 sums.append(acc[pl.ds(line, w), :] + src)
-            for u in range(UNROLL):
+            for u in range(UNROLL_ADD):
                 acc[pl.ds(lines[u], w), :] = sums[u]
             return carry
 
-        lax.fori_loop(0, lax.div(count + UNROLL - 1, UNROLL), body, 0)
+        lax.fori_loop(0, lax.div(count + UNROLL_ADD - 1, UNROLL_ADD), body, 0)
 
     def source(q, carry):
         for part in load(q):
@@ -904,10 +966,11 @@
         c1 = -(-(t * 5 // (8 * n)) // 16) * 16
         c2 = -(-(t // 128) // 16) * 16
         who = lax.axis_index(AXIS)[None].astype(I32)
-        w_up = lax.all_gather(w_up_l, AXIS)
-        w_down = lax.all_gather(w_down_l, AXIS)
+        pieces, spots = gather_weights(n, w_up_l, w_down_l)
         pack, lone_tok, toks, lines, rounds = route(n, vocab, w, c1, c2, token_ids)
-        lists = share(n, pack)
+        lists, across = share(n, pack, pieces[-2], pieces[-1])
+        if n % 4 == 0:
+            pieces, spots = pieces + (across,), spots + ((n // 4, 0),)
         none = jnp.zeros((1,), I32)
 
         def rows_of(rnd):
@@ -919,11 +982,11 @@
             return r + 1, expand(n, r[None], who, toks, lines, *rows_of(r[None]), x_now)
 
         sent = serve(n, c1, c2, none, who, lists, emb_shard)
-        got, most, dh, dot = swap_first(n, others, sent, jnp.full((8, LANES), rounds, I32), grad_out, w_down)
+        got, most, dh, dot, ws = swap_first(n, others, sent, jnp.full((8, LANES), rounds, I32), grad_out, pieces, spots)
         rounds = most[0, 0]
         x = expand(n, none, who, toks, lines, sent, got)
         _, x = lax.while_loop(lambda carry: carry[0] < rounds, more_rows, (jnp.ones((), I32), x))
-        out, dx, dw1, dw2t = mlp(n, 4, x, norm_gain, w_up, w_down, grad_out, dh, dot)
+        out, dx, dw1, dw2t = mlp(n, 4, x, norm_gain, ws, grad_out, dh, dot)
         ids_c = token_ids.reshape(-1, 1, t // 8)
 
         one, many, out, dw1, dw2 = collect(n, c1, c2, vocab, none, pack, lone_tok, ids_c, dx, (out, dw1, dw2t))

time: 250 us -> 236 us (0.944)
  between operations: 15.6 us -> 2.33 us
  Pallas kernels: 211 us -> 206 us
  starting transfers between devices: 0.12 us -> 3.9 us
    ppermute x0 -> x2, starting transfers between devices: none -> 3.9 us  [the longest x1 2.25 us: gather_weights(): behind = lax.ppermute(behind, AXIS, ahead)]
    pallas_call x1, Pallas kernels: 77.5 us -> 73.7 us  [mlp(): pl.pallas_call(functools.partial(mlp_kernel, n, tc), out_shape=(jax.Shape...]
  transfers between devices with their start and end apart: 2 -> 2, of which waited for: 0 -> 0; matrix products, arithmetic and copies ran while one was open for 8% -> 8% of each run, Pallas kernels for 27% -> 0%
where the time goes in v3:
time: 236 us
  Pallas kernels  206 us (87%)
  other arithmetic  16.8 us (7%)
  local copies, waits for them, and re-layouts  5.92 us (3%)
  starting transfers between devices  3.9 us (2%)
    pallas_call x1, Pallas kernels, mlp(): pl.pallas_call(functools.partial(mlp_kernel, n, tc), out_shape=(jax.Shape...  73.7 us
    pallas_call x1, Pallas kernels, swap(): pl.pallas_call(functools.partial(swap_kernel, n, m), out_shape=tuple((jax...  38 us
    pallas_call x1, Pallas kernels, swap_first(): pl.pallas_call(functools.partial(swap_first_kernel, n, others, tc, spots)...  37.4 us
    pallas_call x1, Pallas kernels, place(): pl.pallas_call(functools.partial(place_kernel, n, c1, c2, again), out_sha...  15.4 us
    pallas_call x1, Pallas kernels, share(): pl.pallas_call(functools.partial(share_kernel, n, behind.shape[0] // 2),...  12.6 us
    pallas_call x1, Pallas kernels, expand(): pl.pallas_call(functools.partial(expand_kernel, n, c, again), out_shape=j...  9.99 us
    pallas_call x1, Pallas kernels, collect(): pl.pallas_call(functools.partial(collect_kernel, n, c1, c2, vocab, again)...  9.98 us
    pallas_call x1, Pallas kernels, serve(): pl.pallas_call(functools.partial(serve_kernel, n, c1, c2), out_shape=jax....  8.49 us
  transfers between devices with their start and end apart: 2, of which 0 were waited for; matrix products, arithmetic and copies ran while one was open for 8% of the time, Pallas kernels for 0%

profile of v3, /device:TPU:113, one launch (start us, length us, event | category | flops | bytes accessed | tf_op | source)
XLA Modules:
  0.0 236.0 jit_solution(1871690830774451702)
XLA Ops:
  0.6 1.1 copy.13
  1.7 1.0 pad_maximum_fusion.refs_0_
  2.7 0.0 copy-start
  2.7 2.3 collective-permute-start
  5.0 1.6 collective-permute-start.1
  6.6 5.9 %sort.46 = (s32[4096]{0:T(1024)S(1)}, s32[4096]{0:T(1024)S(1)}) sort(s32[4096]{0:T(1024)} %param.10, s32[4096]{0:T(1024)S(1)} %iota.18), dimensions={0}, to_apply=%region_0.0 | sort | flops 49152 | bytes 65536 | tf_op jit(solution)/shard_map/sort | solution.py:920
  12.5 0.1 fusion.8
  12.6 0.1 convert_bitcast_fusion.1
  12.7 0.1 broadcast_compare_fusion
  12.8 0.1 convert_reduce_fusion
  12.9 0.3 reduce-window.16
  13.2 0.1 slice.57
  13.2 0.1 reduce-window.19
  13.3 0.3 reduce-window.24
  13.6 0.1 slice.59
  13.7 0.1 reduce-window.25
  13.7 0.3 select_reduce_fusion
  14.0 0.7 subtract_reduce_fusion
  14.7 0.1 slice_reduce_fusion
  14.8 0.1 select_reduce_fusion.2
  15.0 0.7 fusion.5
  15.7 0.6 slice.46
  17.6 1.2 reshape.67.g_ref
  18.8 0.6 fusion.6
  19.4 5.9 %sort.47 = (s32[4096]{0:T(1024)}, s32[4096]{0:T(1024)S(1)}, s32[4096]{0:T(1024)S(1)}, s32[4096]{0:T(1024)}) sort(s32[4096]{0:T(1024)S(1)} %get-tuple-element.201, s32[4096]{0:T(1024)S(1)} %get-tuple-element.197, s32[4096]{0:T(1024)S(1)} %get-tuple-element.332, s32[4096]{0:T(1024)S(1)} %iota.21), dimensions={0}, to_apply=%region_2.3 | sort | flops 49152 | bytes 131072 | tf_op jit(solution)/shard_map/sort | solution.py:940
  25.4 0.6 broadcast_add_fusion
  26.0 0.1 concatenate.17.pack.refs_1_
  26.1 0.0 collective-permute-done.behind.refs_1_
  26.1 0.0 copy-start.1
  26.1 0.8 copy-done.1
  26.9 0.0 collective-permute-done.1.before.refs_2_
  26.9 12.6 %share_lists.1 = (s32[49152]{0:T(1024)S(1)}, bf16[512,512]{1,0:T(8,128)(2,1)}) custom-call(s32[6144]{0:T(1024)S(1)} %concatenate.17.pack.refs_1_, bf16[512,512]{1,0:T(8,128)(2,1)} %copy-done.1, bf16[512,512]{1,0:T(8,128)(2,1)} %collective-permute-done.1.before.refs_2_), custom_call_target="tpu_custom_call" | custom-call | tf_op jit(solution)/shard_map/share_lists/pallas_call | solution.py:363
  39.5 8.5 %serve_rows.2.sent.refs_3_ = bf16[8,352,512]{2,1,0:T(8,128)(2,1)} custom-call(s32[1]{0:T(128)} %constant.41.clone.1.rnd_ref.refs_0_, s32[1]{0:T(128)} %bitcast.5.who_ref.refs_0_.refs_1_, s32[49152]{0:T(1024)S(1)} %get-tuple-element.366.lists.refs_2_, bf16[6288,512]{1,0:T(8,128)(2,1)} %table.1), custom_call_target="tpu_custom_call" | custom-call | tf_op jit(solution)/shard_map/serve_rows/pallas_call | solution.py:415
  48.0 0.0 copy-done
  48.0 0.6 broadcast_in_dim.98.need
  48.6 37.4 %swap_first.1 = (bf16[8,352,512]{2,1,0:T(8,128)(2,1)}, s32[8,128]{1,0:T(8,128)}, f32[8,4096,256]{2,1,0:T(8,128)}, bf16[512,4096]{1,0:T(8,128)(2,1)}, bf16[2,4,512,512]{3,2,1,0:T(8,128)(2,1)}) custom-call(bf16[8,352,512]{2,1,0:T(8,128)(2,1)} %serve_rows.2.sent.refs_3_, s32[8,128]{1,0:T(8,128)} %broadcast_in_dim.98.need, bf16[4096,512]{1,0:T(8,128)(2,1)} %do_hbm.3, ...), custom_call_target="tpu_custom_call" | custom-call | tf_op jit(solution)/shard_map/swap_first/pallas_call | solution.py:582
  86.1 1.2 slice.55
  87.3 10.0 %expand_rows.1 = bf16[4096,512]{1,0:T(8,128)(2,1)} custom-call(s32[1]{0:T(128)} %bitcast.5.who_ref.refs_0_.refs_1_, s32[4096]{0:T(1024)} %get-tuple-element.195.refs_1_, s32[4096]{0:T(1024)} %get-tuple-element.186.refs_2_, bf16[8,352,512]{2,1,0:T(8,128)(2,1)} %serve_rows.2.sent.refs_3_, bf16[8,352,512]{2,1,0:T(8,128)(2,1)} %get-tuple-element.130.refs_4_), custom_call_target="tpu_custom_call" | custom-call | tf_op jit(solution)/shard_map/expand_rows/pallas_call | solution.py:677
  97.3 0.7 while.20
  98.0 0.0 copy-start.2
  98.0 73.7 %mlp_block.1 = (bf16[4096,512]{1,0:T(8,128)(2,1)}, bf16[4096,512]{1,0:T(8,128)(2,1)}, f32[512,256]{1,0:T(8,128)}, f32[512,256]{1,0:T(8,128)}) custom-call(bf16[4096,512]{1,0:T(8,128)(2,1)} %get-tuple-element.132.x_hbm, bf16[1,512]{1,0:T(2,128)(2,1)} %reshape.67.g_ref, bf16[2,4,512,512]{3,2,1,0:T(8,128)(2,1)} %get-tuple-element.133.w_hbm, ...), custom_call_target="tpu_custom_call" | custom-call | flops 51539607552 | bytes 41943040 | tf_op jit(solution)/shard_map/mlp_block/pallas_call | solution.py:306
  171.8 0.0 copy-done.2
  171.8 10.0 %collect_rows.1 = (bf16[8,320,512]{2,1,0:T(8,128)(2,1)}, f32[256,512]{1,0:T(8,128)}, bf16[4096,512]{1,0:T(8,128)(2,1)}, f32[512,256]{1,0:T(8,128)}, f32[256,512]{1,0:T(8,128)}) custom-call(s32[1]{0:T(128)} %constant.41.clone.1.rnd_ref.refs_0_, s32[6144]{0:T(1024)S(1)} %concatenate.17.pack.refs_1_, s32[5120]{0:T(1024)S(1)} %concatenate.18.refs_2_, ...), custom_call_target="tpu_custom_call" | custom-call | tf_op jit(solution)/shard_map/collect_rows/pallas_call | solution.py:779
  181.8 38.0 %swap_sums.2 = (bf16[8,320,512]{2,1,0:T(8,128)(2,1)}, f32[8,32,512]{2,1,0:T(8,128)}) custom-call(bf16[8,320,512]{2,1,0:T(8,128)(2,1)} %get-tuple-element.141.refs_0_.refs_3_, f32[8,32,512]{2,1,0:T(8,128)} %bitcast.33), custom_call_target="tpu_custom_call" | custom-call | tf_op jit(solution)/shard_map/swap_sums/pallas_call | solution.py:447
  219.8 15.4 %place_rows.1 = f32[6288,512]{1,0:T(8,128)} custom-call(s32[1]{0:T(128)} %constant.41.clone.1.rnd_ref.refs_0_, s32[1]{0:T(128)} %bitcast.5.who_ref.refs_0_.refs_1_, s32[49152]{0:T(1024)S(1)} %get-tuple-element.388, bf16[8,320,512]{2,1,0:T(8,128)(2,1)} %get-tuple-element.141.refs_0_.refs_3_, f32[8,32,512]{2,1,0:T(8,128)} %bitcast.34, ...), custom_call_target="tpu_custom_call" | custom-call | tf_op jit(solution)/shard_map/place_rows/pallas_call | solution.py:902
  235.3 0.6 while.21
  (10 shorter events, 0.0 us)
Async XLA Ops:
  2.7 45.3 %copy-start = (bf16[512,512]{1,0:T(8,128)(2,1)}, bf16[512,512]{1,0:T(8,128)(2,1)S(1)}, u32[]{:S(2)}) copy-start(bf16[512,512]{1,0:T(8,128)(2,1)S(1)} %pad_maximum_fusion.refs_0_) | copy-start | bytes 1572868
  2.7 23.4 %collective-permute-start = (bf16[512,512]{1,0:T(8,128)(2,1)S(1)}, bf16[512,512]{1,0:T(8,128)(2,1)S(1)}, u32[]{:S(2)}, u32[]{:S(2)}) collective-permute-start(bf16[512,512]{1,0:T(8,128)(2,1)S(1)} %pad_maximum_fusion.refs_0_), channel_id=1, source_target_pairs={{0,2},{1,3},{2,4},{3,5},{4,6},{5,7},{6,0},{7,1},{8,10},{9,11},{10,... | collective-permute-start | bytes 1572872 | tf_op jit(solution)/shard_map/ppermute | solution.py:609
  5.0 21.9 %collective-permute-start.1 = (bf16[512,512]{1,0:T(8,128)(2,1)S(1)}, bf16[512,512]{1,0:T(8,128)(2,1)}, u32[]{:S(2)}, u32[]{:S(2)}) collective-permute-start(bf16[512,512]{1,0:T(8,128)(2,1)S(1)} %pad_maximum_fusion.refs_0_), channel_id=1, source_target_pairs={{0,6},{1,7},{2,0},{3,1},{4,2},{5,3},{6,4},{7,5},{8,14},{9,15},{10,... | collective-permute-start | bytes 1572872 | tf_op jit(solution)/shard_map/ppermute | solution.py:610
  26.1 0.8 copy-start.1
  98.0 73.8 %copy-start.2 = (s32[4096]{0:T(1024)S(1)}, s32[4096]{0:T(1024)}, u32[]{:S(2)}) copy-start(s32[4096]{0:T(1024)} %param.10) | copy-start | bytes 49156
